TPU v7x, 8 devices: a whole 2x2x1 slice. The times are simulated.
8 devices in a mesh: prob: 1 (over z), row: 2 (over y), col: 4 (over x, core).
Axes of the slice: x: 2, y: 2, z: 1, core: 2. Of those that a mesh axis runs over, the one named last changes fastest.
Arguments:
- kernel: bfloat16 [4096, 4096], P('row', 'col')
- cost_mat: bfloat16 [4096, 4096], P('row', 'col')
- src_mass: float32 [4096, 32], P('row', 'prob')
- tgt_mass: float32 [4096, 32], P('col', 'prob')
Outputs:
- output 1: float32 [4096, 32], P('row', 'prob')
- output 2: float32 [4096, 32], P('col', 'prob')
- output 3: float32 [32], P('prob')
All inputs are finite; a program needn't handle non-finite values.
Results may differ from a plain program's by a relative error of at most 0.001.
Values are sent between devices in bfloat16 or wider.
A program may use at most 1 GiB of HBM per device.

v0:
```python
import jax
import jax.numpy as jnp
from jax import lax
from jax.sharding import PartitionSpec as P

SWEEPS = 6


def solution(mesh):
    row_size = mesh.shape["row"]
    col_size = mesh.shape["col"]

    def local_fn(kernel, cost_mat, src_mass, tgt_mass):
        tgt_scale = jnp.ones(tgt_mass.shape, jnp.float32)
        for sweep_idx in range(SWEEPS):
            row_part = jnp.dot(kernel, tgt_scale.astype(jnp.bfloat16), preferred_element_type=jnp.float32)
            src_scale = src_mass / lax.psum(row_part, "col")
            col_part = lax.dot_general(kernel, src_scale.astype(jnp.bfloat16), (((0,), (0,)), ((), ())), preferred_element_type=jnp.float32)
            tgt_scale = tgt_mass / lax.psum(col_part, "row")
        weighted = jnp.dot(kernel * cost_mat, tgt_scale.astype(jnp.bfloat16), preferred_element_type=jnp.float32)
        part_cost = jnp.sum(src_scale * weighted, axis=0)
        mass_norm = float(kernel.shape[0] * row_size * kernel.shape[1] * col_size)
        return src_scale, tgt_scale, lax.psum(part_cost, ("row", "col")) / mass_norm

    return jax.shard_map(local_fn, mesh=mesh, in_specs=(P("row", "col"), P("row", "col"), P("row", "prob"), P("col", "prob")), out_specs=(P("row", "prob"), P("col", "prob"), P("prob")), check_vma=False)
```

profile of v0, /device:TPU:0, one launch (start us, length us, event | category | flops | bytes accessed | tf_op | source)
XLA Modules:
  0.0 351.4 jit_solution(15483178658340176205)
XLA Ops:
  7.2 4.3 %convolution_bitcast_fusion.5 = f32[2048,32]{0,1:T(8,128)} fusion(bf16[2048,1024]{1,0:T(8,128)(2,1)} %param.4), kind=kOutput, calls=%fused_computation.7 | convolution fusion | flops 134217728 | bytes 4456448 | tf_op jit(solution)/shard_map/dot_general | solution.py:16
  11.6 29.6 %all-reduce.13.cloned.1.call-done = f32[2048,32]{0,1:T(8,128)} async-done(((f32[2048,32]{0,1:T(8,128)}), f32[2048,32]{0,1:T(8,128)}) %all-reduce.13.cloned.1.call-update) | async-done | bytes 262160 | tf_op jit(solution)/shard_map/psum | solution.py:17
  45.0 15.9 %all-reduce.15.cloned.1.call-done = f32[1024,32]{0,1:T(8,128)} async-done(((f32[1024,32]{0,1:T(8,128)}), f32[1024,32]{0,1:T(8,128)}) %all-reduce.15.cloned.1.call-update) | async-done | bytes 131088 | tf_op jit(solution)/shard_map/psum | solution.py:19
  60.9 4.3 %convolution_bitcast_fusion.4 = f32[2048,32]{0,1:T(8,128)} fusion(bf16[2048,1024]{1,0:T(8,128)(2,1)} %param.4, f32[1024,32]{0,1:T(8,128)S(1)} %copy-done.1, f32[1024,32]{0,1:T(8,128)} %all-reduce.15.cloned.1.call-done), kind=kOutput, calls=%fused_computation.6 | convolution fusion | flops 134283264 | bytes 4718592 | tf_op jit(solution)/shard_map/dot_general | solution.py:16
  65.3 26.7 %all-reduce.17.cloned.1.call-done = f32[2048,32]{0,1:T(8,128)} async-done(((f32[2048,32]{0,1:T(8,128)}), f32[2048,32]{0,1:T(8,128)}) %all-reduce.17.cloned.1.call-update) | async-done | bytes 262160 | tf_op jit(solution)/shard_map/psum | solution.py:17
  92.0 3.8 %convolution_bitcast_fusion.10 = f32[1024,32]{0,1:T(8,128)} fusion(bf16[2048,1024]{1,0:T(8,128)(2,1)} %param.4, f32[2048,32]{0,1:T(8,128)S(1)} %copy-done, f32[2048,32]{0,1:T(8,128)} %all-reduce.17.cloned.1.call-done), kind=kOutput, calls=%fused_computation.14 | convolution fusion | flops 134348800 | bytes 4849664 | tf_op jit(solution)/shard_map/dot_general | solution.py:18
  95.8 15.9 %all-reduce.19.cloned.1.call-done = f32[1024,32]{0,1:T(8,128)} async-done(((f32[1024,32]{0,1:T(8,128)}), f32[1024,32]{0,1:T(8,128)}) %all-reduce.19.cloned.1.call-update) | async-done | bytes 131088 | tf_op jit(solution)/shard_map/psum | solution.py:19
  111.7 4.3 %convolution_bitcast_fusion.3 = f32[2048,32]{0,1:T(8,128)} fusion(bf16[2048,1024]{1,0:T(8,128)(2,1)} %param.4, f32[1024,32]{0,1:T(8,128)S(1)} %copy-done.1, f32[1024,32]{0,1:T(8,128)} %all-reduce.19.cloned.1.call-done), kind=kOutput, calls=%fused_computation.5 | convolution fusion | flops 134283264 | bytes 4718592 | tf_op jit(solution)/shard_map/dot_general | solution.py:16
  116.1 26.7 %all-reduce.21.cloned.1.call-done = f32[2048,32]{0,1:T(8,128)} async-done(((f32[2048,32]{0,1:T(8,128)}), f32[2048,32]{0,1:T(8,128)}) %all-reduce.21.cloned.1.call-update) | async-done | bytes 262160 | tf_op jit(solution)/shard_map/psum | solution.py:17
  146.6 15.9 %all-reduce.23.cloned.1.call-done = f32[1024,32]{0,1:T(8,128)} async-done(((f32[1024,32]{0,1:T(8,128)}), f32[1024,32]{0,1:T(8,128)}) %all-reduce.23.cloned.1.call-update) | async-done | bytes 131088 | tf_op jit(solution)/shard_map/psum | solution.py:19
  162.5 4.3 %convolution_bitcast_fusion.2 = f32[2048,32]{0,1:T(8,128)} fusion(bf16[2048,1024]{1,0:T(8,128)(2,1)} %param.4, f32[1024,32]{0,1:T(8,128)S(1)} %copy-done.1, f32[1024,32]{0,1:T(8,128)} %all-reduce.23.cloned.1.call-done), kind=kOutput, calls=%fused_computation.4 | convolution fusion | flops 134283264 | bytes 4718592 | tf_op jit(solution)/shard_map/dot_general | solution.py:16
  166.9 26.7 %all-reduce.25.cloned.1.call-done = f32[2048,32]{0,1:T(8,128)} async-done(((f32[2048,32]{0,1:T(8,128)}), f32[2048,32]{0,1:T(8,128)}) %all-reduce.25.cloned.1.call-update) | async-done | bytes 262160 | tf_op jit(solution)/shard_map/psum | solution.py:17
  193.6 3.7 %convolution_bitcast_fusion.8 = f32[1024,32]{0,1:T(8,128)} fusion(bf16[2048,1024]{1,0:T(8,128)(2,1)} %param.4, f32[2048,32]{0,1:T(8,128)S(1)} %copy-done, f32[2048,32]{0,1:T(8,128)} %all-reduce.25.cloned.1.call-done), kind=kOutput, calls=%fused_computation.12 | convolution fusion | flops 134348800 | bytes 4849664 | tf_op jit(solution)/shard_map/dot_general | solution.py:18
  197.4 15.9 %all-reduce.27.cloned.1.call-done = f32[1024,32]{0,1:T(8,128)} async-done(((f32[1024,32]{0,1:T(8,128)}), f32[1024,32]{0,1:T(8,128)}) %all-reduce.27.cloned.1.call-update) | async-done | bytes 131088 | tf_op jit(solution)/shard_map/psum | solution.py:19
  213.3 4.3 %convolution_bitcast_fusion.1 = f32[2048,32]{0,1:T(8,128)} fusion(bf16[2048,1024]{1,0:T(8,128)(2,1)} %param.4, f32[1024,32]{0,1:T(8,128)S(1)} %copy-done.1, f32[1024,32]{0,1:T(8,128)} %all-reduce.27.cloned.1.call-done), kind=kOutput, calls=%fused_computation.3 | convolution fusion | flops 134283264 | bytes 4718592 | tf_op jit(solution)/shard_map/dot_general | solution.py:16
  217.7 26.7 %all-reduce.29.cloned.1.call-done = f32[2048,32]{0,1:T(8,128)} async-done(((f32[2048,32]{0,1:T(8,128)}), f32[2048,32]{0,1:T(8,128)}) %all-reduce.29.cloned.1.call-update) | async-done | bytes 262160 | tf_op jit(solution)/shard_map/psum | solution.py:17
  244.4 3.8 %convolution_bitcast_fusion.7 = f32[1024,32]{0,1:T(8,128)} fusion(bf16[2048,1024]{1,0:T(8,128)(2,1)} %param.4, f32[2048,32]{0,1:T(8,128)S(1)} %copy-done, f32[2048,32]{0,1:T(8,128)} %all-reduce.29.cloned.1.call-done), kind=kOutput, calls=%fused_computation.11 | convolution fusion | flops 134348800 | bytes 4849664 | tf_op jit(solution)/shard_map/dot_general | solution.py:18
  248.2 15.9 %all-reduce.31.cloned.1.call-done = f32[1024,32]{0,1:T(8,128)} async-done(((f32[1024,32]{0,1:T(8,128)}), f32[1024,32]{0,1:T(8,128)}) %all-reduce.31.cloned.1.call-update) | async-done | bytes 131088 | tf_op jit(solution)/shard_map/psum | solution.py:19
  264.1 4.3 %convolution_bitcast_fusion = f32[2048,32]{0,1:T(8,128)} fusion(bf16[2048,1024]{1,0:T(8,128)(2,1)} %param.4, f32[1024,32]{0,1:T(8,128)S(1)} %copy-done.1, f32[1024,32]{0,1:T(8,128)} %all-reduce.31.cloned.1.call-done), kind=kOutput, calls=%fused_computation.2 | convolution fusion | flops 134283264 | bytes 4718592 | tf_op jit(solution)/shard_map/dot_general | solution.py:16
  268.5 26.7 %all-reduce.33.cloned.1.call-done = f32[2048,32]{0,1:T(8,128)} async-done(((f32[2048,32]{0,1:T(8,128)}), f32[2048,32]{0,1:T(8,128)}) %all-reduce.33.cloned.1.call-update) | async-done | bytes 262160 | tf_op jit(solution)/shard_map/psum | solution.py:17
  296.2 3.8 %convolution_bitcast_fusion.6 = f32[1024,32]{0,1:T(8,128)} fusion(bf16[2048,1024]{1,0:T(8,128)(2,1)} %param.4, f32[2048,32]{0,1:T(8,128)S(1)} %div.52), kind=kOutput, calls=%fused_computation.10 | convolution fusion | flops 134283264 | bytes 4587520 | tf_op jit(solution)/shard_map/dot_general | solution.py:18
  300.0 15.9 %all-reduce.35.cloned.1.call-done = f32[1024,32]{0,1:T(8,128)} async-done(((f32[1024,32]{0,1:T(8,128)}), f32[1024,32]{0,1:T(8,128)}) %all-reduce.35.cloned.1.call-update) | async-done | bytes 131088 | tf_op jit(solution)/shard_map/psum | solution.py:19
  316.9 4.9 %fusion.5 = f32[32]{0:T(128)S(1)} fusion(f32[2048,32]{0,1:T(8,128)S(1)} %div.52, bf16[2048,1024]{1,0:T(8,128)(2,1)} %param.4, bf16[2048,1024]{1,0:T(8,128)(2,1)} %param.5, f32[1024,32]{0,1:T(8,128)S(1)} %div.53), kind=kOutput, calls=%fused_computation.9 | convolution fusion | flops 136478688 | bytes 8781952 | tf_op jit(solution)/shard_map/dot_general | solution.py:20
  321.8 22.2 %psum.103 = f32[32]{0:T(128)S(1)} all-reduce(f32[32]{0:T(128)S(1)} %fusion.5), channel_id=1, replica_groups=mesh['prob'=1,'row'=2,'col'=4] {'row','col'}, use_global_device_ids=true, to_apply=%region_13.0 | all-reduce | flops 32 | bytes 256 | tf_op jit(solution)/shard_map/psum | solution.py:23
  (37 shorter events, 10.6 us)
Async XLA Ops:
  7.2 34.0 %copy-start = (f32[2048,32]{0,1:T(8,128)S(1)}, f32[2048,32]{0,1:T(8,128)}, u32[]{:S(2)}) copy-start(f32[2048,32]{0,1:T(8,128)} %param.6) | copy-start | bytes 786436
  7.2 53.7 %copy-start.1 = (f32[1024,32]{0,1:T(8,128)S(1)}, f32[1024,32]{0,1:T(8,128)}, u32[]{:S(2)}) copy-start(f32[1024,32]{0,1:T(8,128)} %param.7) | copy-start | bytes 393220
  7.2 34.0 %all-reduce.13.cloned.1.call-start = ((), (), s32[]{:S(2)}) async-start(), calls=%async_computation | async-start | bytes 524288 | tf_op jit(solution)/shard_map/psum | solution.py:17
  11.6 49.3 %all-reduce.15.cloned.1.call-start = ((), (), s32[]{:S(2)}) async-start(), calls=%async_computation.1 | async-start | bytes 262144 | tf_op jit(solution)/shard_map/psum | solution.py:19
  44.9 47.0 %all-reduce.17.cloned.1.call-start = ((), (), s32[]{:S(2)}) async-start(), calls=%async_computation.2 | async-start | bytes 524288 | tf_op jit(solution)/shard_map/psum | solution.py:17
  65.2 46.5 %all-reduce.19.cloned.1.call-start = ((), (), s32[]{:S(2)}) async-start(), calls=%async_computation.3 | async-start | bytes 262144 | tf_op jit(solution)/shard_map/psum | solution.py:19
  95.8 47.0 %all-reduce.21.cloned.1.call-start = ((), (), s32[]{:S(2)}) async-start(), calls=%async_computation.4 | async-start | bytes 524288 | tf_op jit(solution)/shard_map/psum | solution.py:17
  116.0 46.5 %all-reduce.23.cloned.1.call-start = ((), (), s32[]{:S(2)}) async-start(), calls=%async_computation.5 | async-start | bytes 262144 | tf_op jit(solution)/shard_map/psum | solution.py:19
  146.6 47.0 %all-reduce.25.cloned.1.call-start = ((), (), s32[]{:S(2)}) async-start(), calls=%async_computation.6 | async-start | bytes 524288 | tf_op jit(solution)/shard_map/psum | solution.py:17
  166.8 46.5 %all-reduce.27.cloned.1.call-start = ((), (), s32[]{:S(2)}) async-start(), calls=%async_computation.7 | async-start | bytes 262144 | tf_op jit(solution)/shard_map/psum | solution.py:19
  197.4 47.0 %all-reduce.29.cloned.1.call-start = ((), (), s32[]{:S(2)}) async-start(), calls=%async_computation.8 | async-start | bytes 524288 | tf_op jit(solution)/shard_map/psum | solution.py:17
  217.6 46.5 %all-reduce.31.cloned.1.call-start = ((), (), s32[]{:S(2)}) async-start(), calls=%async_computation.9 | async-start | bytes 262144 | tf_op jit(solution)/shard_map/psum | solution.py:19
  248.2 47.0 %all-reduce.33.cloned.1.call-start = ((), (), s32[]{:S(2)}) async-start(), calls=%async_computation.10 | async-start | bytes 524288 | tf_op jit(solution)/shard_map/psum | solution.py:17
  268.4 47.5 %all-reduce.35.cloned.1.call-start = ((), (), s32[]{:S(2)}) async-start(), calls=%async_computation.11 | async-start | bytes 262144 | tf_op jit(solution)/shard_map/psum | solution.py:19
  296.2 25.6 %copy-start.2 = (f32[2048,32]{0,1:T(8,128)}, f32[2048,32]{0,1:T(8,128)S(1)}, u32[]{:S(2)}) copy-start(f32[2048,32]{0,1:T(8,128)S(1)} %div.52) | copy-start | bytes 786436
  316.9 4.9 %copy-start.3 = (f32[1024,32]{0,1:T(8,128)}, f32[1024,32]{0,1:T(8,128)S(1)}, u32[]{:S(2)}) copy-start(f32[1024,32]{0,1:T(8,128)S(1)} %div.53) | copy-start | bytes 393220
Sparse Core Ops, SparseCore 0:
  11.7 29.4 all-reduce.12
  45.1 15.7 all-reduce.14
  65.3 26.5 all-reduce.16
  95.9 15.7 all-reduce.18
  116.2 26.5 all-reduce.20
  146.7 15.7 all-reduce.22
  167.0 26.5 all-reduce.24
  197.5 15.7 all-reduce.26
  217.8 26.5 all-reduce.28
  248.3 15.7 all-reduce.30
  268.6 26.5 all-reduce.32
  300.1 15.7 all-reduce.34
where the time goes:
time: 352 us; the launch traced here: 351 us
  waiting for transfers between devices  259 us (74%)
  matrix products  53.3 us (15%)
  blocking collectives  22.2 us (6%)
  between operations  14.3 us (4%)
    psum x6, waiting for transfers between devices, local_fn(): src_scale = src_mass / lax.psum(row_part, 'col')  163 us
    psum x6, waiting for transfers between devices, local_fn(): tgt_scale = tgt_mass / lax.psum(col_part, 'row')  95.4 us
    dot_general x6, matrix products, local_fn(): jnp.dot(kernel, tgt_scale.astype(jnp.bfloat16), preferred_element_type=jn...  25.9 us
    dot_general x6, matrix products, local_fn(): lax.dot_general(kernel, src_scale.astype(jnp.bfloat16), (((0,), (0,)), ((...  22.5 us
    psum x1, blocking collectives, local_fn(): lax.psum(part_cost, ('row', 'col')) / mass_norm  22.2 us
  transfers between devices with their start and end apart: 12, of which 12 were waited for; matrix products, arithmetic and copies ran while one was open for 0% of the time, Pallas kernels for 0%

commit v1 on v0

v1 whole, which is shorter than its diff:
```python
import jax
import jax.numpy as jnp
from jax import lax
from jax.experimental import pallas as pl
from jax.experimental.pallas import tpu as pltpu
from jax.sharding import PartitionSpec as P

SWEEPS = 6
F32 = jnp.float32
BF16 = jnp.bfloat16
MESH = pl.DeviceIdType.MESH


def sinkhorn_kernel(n_chunk, norm, k_hbm, c_hbm, a_hbm, b_hbm, u_hbm, v_hbm, cost_ref,
                    k_buf, kt_buf, c_buf, kct_buf, a_buf, b_buf, ub_buf, acc,
                    s_out, s_in, t_out, t_in, s0_buf, u_out, v_all, v_out, cost_part, cost_all,
                    k_sem, kp_send, kp_recv, c_sem, ab_sem, bp_sem, s0_send, s0_recv,
                    s_send, s_recv, t_send, t_recv, fin_sem, cs_send, cs_recv, out_sem):
    rows, half = k_hbm.shape
    cols = 2 * half
    rw = rows // n_chunk
    cw = cols // n_chunk
    per_half = n_chunk // 2
    nq = a_buf.shape[0]
    row = lax.axis_index("row")
    col = lax.axis_index("col")
    prob = lax.axis_index("prob")
    x = col // 2
    core = col % 2
    grp = (core + x + row) % 2
    me = row * 4 + col
    mine = pl.ds(pl.multiple_of(grp * nq, nq), nq)
    other = pl.ds(pl.multiple_of((1 - grp) * nq, nq), nq)

    def dev(r, c):
        return (prob, r, c)

    partner = dev(row, 2 * x + 1 - core)
    x_peer = dev(row, 2 * (1 - x) + 1 - core)
    y_peer = dev(1 - row, 2 * x + 1 - core)

    def remote(src, dst, send, recv, to):
        return pltpu.make_async_remote_copy(src_ref=src, dst_ref=dst, send_sem=send, recv_sem=recv,
                                            device_id=to, device_id_type=MESH)

    def krows(i):
        return pl.ds(i * rw, rw)

    k_load = [pltpu.make_async_copy(k_hbm.at[krows(i)], k_buf.at[core, krows(i)], k_sem.at[i]) for i in range(n_chunk)]
    c_load = [pltpu.make_async_copy(c_hbm.at[krows(i)], c_buf.at[krows(i)], c_sem.at[i]) for i in range(n_chunk)]
    a_load = pltpu.make_async_copy(a_hbm.at[mine], a_buf, ab_sem.at[0])
    b_load = pltpu.make_async_copy(b_hbm.at[mine], b_buf.at[core], ab_sem.at[1])
    for d in k_load:
        d.start()
    a_load.start()
    b_load.start()
    for d in c_load:
        d.start()

    barrier = pltpu.get_barrier_semaphore()
    for dr in range(2):
        for dc in range(4):
            if dr or dc:
                pl.semaphore_signal(barrier, inc=1, device_id=dev((row + dr) % 2, (col + dc) % 4), device_id_type=MESH)

    def transpose_rows(h, i):
        blk = 256
        def body(n, carry):
            jo = pl.multiple_of(n * blk, blk)
            for ii in range(rw // blk):
                kt_buf[pl.ds(pl.multiple_of(h * half + jo, blk), blk), pl.ds(i * rw + ii * blk, blk)] = (
                    k_buf[h, pl.ds(i * rw + ii * blk, blk), pl.ds(jo, blk)].T)
            return carry
        lax.fori_loop(0, half // blk, body, 0)

    ones = jnp.ones((nq, half), BF16)
    own_half = pl.ds(pl.multiple_of(core * half, half), half)
    for i in range(n_chunk):
        k_load[i].wait()
        transpose_rows(core, i)
        part = jnp.dot(ones, kt_buf[own_half, krows(i)], preferred_element_type=F32)
        for n in range(rw // 128):
            r = i * (rw // 128) + n
            s0_buf[col, r:r + 1, :] = part[0:1, n * 128:(n + 1) * 128]

    pl.semaphore_wait(barrier, 7)
    s0_copies = []
    for n in range(1, 4):
        d = remote(s0_buf.at[col], s0_buf.at[col], s0_send.at[n], s0_recv.at[n], dev(row, (col + n) % 4))
        d.start()
        s0_copies.append(d)
    k_push = [remote(k_buf.at[core, krows(i)], k_buf.at[core, krows(i)], kp_send.at[i], kp_recv.at[i], partner) for i in range(n_chunk)]
    for d in k_push:
        d.start()
    b_push = remote(b_hbm.at[other], b_buf.at[core], bp_sem.at[0], bp_sem.at[1], partner)
    b_push.start()

    for i in range(n_chunk):
        c_load[i].wait()
        blk = 256
        def body(n, carry):
            jo = pl.multiple_of(n * blk, blk)
            for ii in range(rw // blk):
                rs = pl.ds(i * rw + ii * blk, blk)
                kct_buf[pl.ds(jo, blk), rs] = (k_buf[core, rs, pl.ds(jo, blk)] * c_buf[rs, pl.ds(jo, blk)]).T
            return carry
        lax.fori_loop(0, half // blk, body, 0)

    a_load.wait()
    b_load.wait()
    for n in range(1, 4):
        frm = (col + 4 - n) % 4
        remote(s0_buf.at[frm], s0_buf.at[frm], s0_send.at[n], s0_recv.at[n], dev(row, frm)).wait_recv()
    s0 = (s0_buf[0] + s0_buf[1]) + (s0_buf[2] + s0_buf[3])
    for r in range(rows // 128):
        cs = slice(r * 128, (r + 1) * 128)
        ub_buf[:, cs] = (a_buf[:, cs] / s0[r:r + 1, :]).astype(BF16)

    def t_copy(par, o):
        return remote(t_out.at[o], t_in.at[par, o], t_send.at[o], t_recv.at[par, o], y_peer)

    def s_copy(par, o):
        return remote(s_out.at[o], s_in.at[par, o], s_send.at[o], s_recv.at[par, o], x_peer)

    def send_t_half(h):
        for n in range(per_half):
            o = h * per_half + n
            t_out[o] = jnp.dot(ub_buf[...], k_buf[h, :, n * cw:(n + 1) * cw], preferred_element_type=F32)
            t_copy(0, o).start()

    send_t_half(core)
    for i in range(n_chunk):
        remote(k_buf.at[1 - core, krows(i)], k_buf.at[1 - core, krows(i)], kp_send.at[i], kp_recv.at[i], partner).wait_recv()
    remote(b_hbm.at[other], b_buf.at[1 - core], bp_sem.at[0], bp_sem.at[1], partner).wait_recv()
    send_t_half(1 - core)
    for i in range(n_chunk):
        transpose_rows(1 - core, i)

    def sweep(t, carry):
        par_in = (t + 1) % 2
        par = t % 2
        for c in range(n_chunk):
            t_copy(par_in, c).wait()
            v = b_buf[c // per_half, :, (c % per_half) * cw:(c % per_half + 1) * cw] / (t_out[c] + t_in[par_in, c])
            vb = v.astype(BF16)
            w = slice(c * cw, (c + 1) * cw)
            if c < n_chunk - 1:
                prod = jnp.dot(vb, kt_buf[w, :], preferred_element_type=F32)
                acc[...] = prod if c == 0 else acc[...] + prod
            else:
                for o in range(n_chunk):
                    oc = slice(o * rw, (o + 1) * rw)
                    s_out[o] = acc[:, oc] + jnp.dot(vb, kt_buf[w, oc], preferred_element_type=F32)
                    s_copy(par, o).start()
        for c in range(n_chunk):
            s_copy(par, c).wait()
            w = slice(c * rw, (c + 1) * rw)
            u = a_buf[:, w] / (s_out[c] + s_in[par, c])
            u_out[mine, w] = u
            ub = u.astype(BF16)
            if c < n_chunk - 1:
                for h in range(2):
                    hc = slice(h * half, (h + 1) * half)
                    prod = jnp.dot(ub, k_buf[h, w, :], preferred_element_type=F32)
                    acc[:, hc] = prod if c == 0 else acc[:, hc] + prod
            else:
                for o in range(n_chunk):
                    oc = slice(o * cw, (o + 1) * cw)
                    hc = slice((o % per_half) * cw, (o % per_half + 1) * cw)
                    t_out[o] = acc[:, oc] + jnp.dot(ub, k_buf[o // per_half, w, hc], preferred_element_type=F32)
                    t_copy(par, o).start()
        return carry

    lax.fori_loop(1, SWEEPS, sweep, 0)

    u_push = remote(u_out.at[mine], u_out.at[mine], fin_sem.at[0], fin_sem.at[1], partner)
    u_push.start()
    last = (SWEEPS - 1) % 2
    for c in range(n_chunk):
        t_copy(last, c).wait()
        cs = slice((c % per_half) * cw, (c % per_half + 1) * cw)
        v_all[c // per_half, :, cs] = b_buf[c // per_half, :, cs] / (t_out[c] + t_in[last, c])
    v_push = remote(v_all.at[1 - core], v_out.at[mine], fin_sem.at[2], fin_sem.at[3], partner)
    v_push.start()
    v_own = v_all[core]
    v_out[mine] = v_own

    def cost_rows(v, who):
        w = jnp.dot(v.astype(BF16), kct_buf[...], preferred_element_type=F32) * u_out[who]
        tot = w[:, 0:128]
        for n in range(1, rows // 128):
            tot = tot + w[:, n * 128:(n + 1) * 128]
        cost_part[who] = tot

    cost_part[...] = jnp.zeros_like(cost_part)
    cost_rows(v_own, mine)
    remote(u_out.at[other], u_out.at[other], fin_sem.at[0], fin_sem.at[1], partner).wait_recv()
    u_push.wait_send()
    u_store = pltpu.make_async_copy(u_out, u_hbm, out_sem.at[0])
    u_store.start()
    remote(v_all.at[core], v_out.at[other], fin_sem.at[2], fin_sem.at[3], partner).wait_recv()
    v_push.wait_send()
    v_store = pltpu.make_async_copy(v_out, v_hbm, out_sem.at[1])
    v_store.start()
    cost_rows(v_out[other], other)
    cost_all[me] = jnp.sum(cost_part[...].T, axis=0, keepdims=True)
    cost_copies = []
    for dr in range(2):
        for dc in range(4):
            if dr or dc:
                n = dr * 4 + dc
                d = remote(cost_all.at[me], cost_all.at[me], cs_send.at[n], cs_recv.at[n], dev((row + dr) % 2, (col + dc) % 4))
                d.start()
                cost_copies.append((n, (row + dr) % 2, (col + 4 - dc) % 4, d))
    for d in s0_copies + k_push:
        d.wait_send()
    b_push.wait_send()
    for n, fr, fc, d in cost_copies:
        f = fr * 4 + fc
        remote(cost_all.at[f], cost_all.at[f], cs_send.at[n], cs_recv.at[n], dev(fr, fc)).wait_recv()
    total = cost_all[0]
    for n in range(1, 8):
        total = total + cost_all[n]
    cost_ref[...] = total[:, :cost_ref.shape[1]] * norm
    for n, fr, fc, d in cost_copies:
        d.wait_send()
    u_store.wait()
    v_store.wait()


def solution(mesh):
    n_chunk = 4

    def local_fn(kernel, cost_mat, src_mass, tgt_mass):
        rows, half = kernel.shape
        nprob = src_mass.shape[1]
        nq = nprob // 2
        cols = 2 * half
        rw, cw = rows // n_chunk, cols // n_chunk
        norm = 1.0 / float(rows * mesh.shape["row"] * half * mesh.shape["col"])
        any_spec = pl.BlockSpec(memory_space=pl.ANY)
        dma = pltpu.SemaphoreType.DMA
        u_t, v_t, cost = pl.pallas_call(
            lambda *refs: sinkhorn_kernel(n_chunk, norm, *refs),
            out_shape=(jax.ShapeDtypeStruct((nprob, rows), F32), jax.ShapeDtypeStruct((nprob, half), F32),
                       jax.ShapeDtypeStruct((1, nprob), F32)),
            in_specs=[any_spec] * 4,
            out_specs=(any_spec, any_spec, pl.BlockSpec(memory_space=pltpu.VMEM)),
            scratch_shapes=[
                pltpu.VMEM((2, rows, half), BF16),
                pltpu.VMEM((cols, rows), BF16),
                pltpu.VMEM((rows, half), BF16),
                pltpu.VMEM((half, rows), BF16),
                pltpu.VMEM((nq, rows), F32),
                pltpu.VMEM((2, nq, half), F32),
                pltpu.VMEM((nq, rows), BF16),
                pltpu.VMEM((nq, max(rows, cols)), F32),
                pltpu.VMEM((n_chunk, nq, rw), F32),
                pltpu.VMEM((2, n_chunk, nq, rw), F32),
                pltpu.VMEM((n_chunk, nq, cw), F32),
                pltpu.VMEM((2, n_chunk, nq, cw), F32),
                pltpu.VMEM((4, rows // 128, 128), F32),
                pltpu.VMEM((nprob, rows), F32),
                pltpu.VMEM((2, nq, half), F32),
                pltpu.VMEM((nprob, half), F32),
                pltpu.VMEM((128, 128), F32),
                pltpu.VMEM((8, 1, 128), F32),
                dma((n_chunk,)), dma((n_chunk,)), dma((n_chunk,)), dma((n_chunk,)), dma((2,)), dma((2,)), dma((4,)), dma((4,)),
                dma((n_chunk,)), dma((2, n_chunk)), dma((n_chunk,)), dma((2, n_chunk)), dma((4,)), dma((8,)), dma((8,)), dma((2,)),
            ],
            compiler_params=pltpu.CompilerParams(collective_id=0, has_side_effects=True, vmem_limit_bytes=60 * 1024 * 1024),
            name="sinkhorn",
        )(kernel, cost_mat, src_mass.T, tgt_mass.T)
        return u_t.T, v_t.T, cost.reshape(nprob)

    return jax.shard_map(local_fn, mesh=mesh, in_specs=(P("row", "col"), P("row", "col"), P("row", "prob"), P("col", "prob")), out_specs=(P("row", "prob"), P("col", "prob"), P("prob")), check_vma=False)
```

time: 352 us -> 77 us (0.22)
  waiting for transfers between devices: 259 us -> 0 us
  Pallas kernels: 0 us -> 71.9 us
  matrix products: 53.3 us -> 0 us
  blocking collectives: 22.2 us -> 0 us
  between operations: 14.3 us -> 0.64 us
  local copies, waits for them, and re-layouts: 0.02 us -> 4.36 us
    psum x12 -> x0, waiting for transfers between devices: 258 us -> none  [the longest x6 163 us: local_fn(): src_scale = src_mass / lax.psum(row_part, 'col')]
    pallas_call x0 -> x1, Pallas kernels: none -> 71.9 us  [local_fn(): pl.pallas_call(lambda *refs: sinkhorn_kernel(n_chunk, norm, *refs), out_s...]
    dot_general x13 -> x0, matrix products: 53.3 us -> none  [the longest x6 25.9 us: local_fn(): jnp.dot(kernel, tgt_scale.astype(jnp.bfloat16), preferred_element_type=jn...]
    psum x1 -> x0, blocking collectives: 22.2 us -> none  [local_fn(): lax.psum(part_cost, ('row', 'col')) / mass_norm]
    unnamed x8 -> x3, local copies, waits for them, and re-layouts: 0.02 us -> 4.36 us
  transfers between devices with their start and end apart: 12 -> 0, of which waited for: 12 -> 0; matrix products, arithmetic and copies ran while one was open for 0% -> 0% of each run, Pallas kernels for 0% -> 0%
where the time goes in v1:
time: 77 us; the launch traced here: 76.9 us
  Pallas kernels  71.9 us (93%)
  local copies, waits for them, and re-layouts  4.36 us (6%)
    pallas_call x1, Pallas kernels, local_fn(): pl.pallas_call(lambda *refs: sinkhorn_kernel(n_chunk, norm, *refs), out_s...  71.9 us
    unnamed x3, local copies, waits for them, and re-layouts  4.36 us

profile of v1, /device:TPU:0, one launch (start us, length us, event | category | flops | bytes accessed | tf_op | source)
XLA Modules:
  0.0 76.9 jit_solution(5552363287762025095)
XLA Ops:
  0.6 71.9 %sinkhorn.1 = (f32[32,2048]{1,0:T(8,128)}, f32[32,1024]{1,0:T(8,128)}, f32[1,32]{1,0:T(1,128)}) custom-call(bf16[2048,1024]{1,0:T(8,128)(2,1)} %refs_0_.1, bf16[2048,1024]{1,0:T(8,128)(2,1)} %refs_1_.1, f32[32,2048]{1,0:T(8,128)} %bitcast.5, f32[32,1024]{1,0:T(8,128)} %bitcast.7), custom_call_target="tpu_custom_call" | custom-call | tf_op jit(solution)/shard_map/sinkhorn/pallas_call | solution.py:243
  72.5 1.7 %copy.10 = f32[2048,32]{0,1:T(8,128)} copy(f32[2048,32]{0,1:T(8,128)} %bitcast.6) | data formatting | bytes 524288
  74.2 1.6 %copy.11 = f32[1024,32]{0,1:T(8,128)} copy(f32[1024,32]{0,1:T(8,128)} %bitcast.8) | data formatting | bytes 262144
  75.8 1.1 %copy.12 = f32[32]{0:T(128)} copy(f32[32]{0:T(128)} %bitcast.9) | data formatting | bytes 256

commit v2 on v1

--- a/solution.py
+++ b/solution.py
@@ -73,38 +73,37 @@
             return carry
         lax.fori_loop(0, half // blk, body, 0)
 
+    def build_kct():
+        for i in range(n_chunk):
+            c_load[i].wait()
+            blk = 256
+            def body(n, carry):
+                jo = pl.multiple_of(n * blk, blk)
+                for ii in range(rw // blk):
+                    rs = pl.ds(i * rw + ii * blk, blk)
+                    kct_buf[pl.ds(jo, blk), rs] = (k_buf[core, rs, pl.ds(jo, blk)] * c_buf[rs, pl.ds(jo, blk)]).T
+                return carry
+            lax.fori_loop(0, half // blk, body, 0)
+
+    pl.semaphore_wait(barrier, 7)
     ones = jnp.ones((nq, half), BF16)
-    own_half = pl.ds(pl.multiple_of(core * half, half), half)
+    k_push = [remote(k_buf.at[core, krows(i)], k_buf.at[core, krows(i)], kp_send.at[i], kp_recv.at[i], partner) for i in range(n_chunk)]
     for i in range(n_chunk):
         k_load[i].wait()
-        transpose_rows(core, i)
-        part = jnp.dot(ones, kt_buf[own_half, krows(i)], preferred_element_type=F32)
+        k_push[i].start()
+        part = lax.dot_general(ones, k_buf[core, krows(i)], (((1,), (1,)), ((), ())), preferred_element_type=F32)
         for n in range(rw // 128):
             r = i * (rw // 128) + n
             s0_buf[col, r:r + 1, :] = part[0:1, n * 128:(n + 1) * 128]
-
-    pl.semaphore_wait(barrier, 7)
     s0_copies = []
     for n in range(1, 4):
         d = remote(s0_buf.at[col], s0_buf.at[col], s0_send.at[n], s0_recv.at[n], dev(row, (col + n) % 4))
         d.start()
         s0_copies.append(d)
-    k_push = [remote(k_buf.at[core, krows(i)], k_buf.at[core, krows(i)], kp_send.at[i], kp_recv.at[i], partner) for i in range(n_chunk)]
-    for d in k_push:
-        d.start()
     b_push = remote(b_hbm.at[other], b_buf.at[core], bp_sem.at[0], bp_sem.at[1], partner)
     b_push.start()
-
     for i in range(n_chunk):
-        c_load[i].wait()
-        blk = 256
-        def body(n, carry):
-            jo = pl.multiple_of(n * blk, blk)
-            for ii in range(rw // blk):
-                rs = pl.ds(i * rw + ii * blk, blk)
-                kct_buf[pl.ds(jo, blk), rs] = (k_buf[core, rs, pl.ds(jo, blk)] * c_buf[rs, pl.ds(jo, blk)]).T
-            return carry
-        lax.fori_loop(0, half // blk, body, 0)
+        transpose_rows(core, i)
 
     a_load.wait()
     b_load.wait()
@@ -129,12 +128,24 @@
             t_copy(0, o).start()
 
     send_t_half(core)
+    build_kct()
     for i in range(n_chunk):
         remote(k_buf.at[1 - core, krows(i)], k_buf.at[1 - core, krows(i)], kp_send.at[i], kp_recv.at[i], partner).wait_recv()
     remote(b_hbm.at[other], b_buf.at[1 - core], bp_sem.at[0], bp_sem.at[1], partner).wait_recv()
+
+    def rest_of_kt():
+        for i in range(n_chunk):
+            transpose_rows(1 - core, i)
+
+    @pl.when(grp == 1)
+    def _():
+        rest_of_kt()
+
     send_t_half(1 - core)
-    for i in range(n_chunk):
-        transpose_rows(1 - core, i)
+
+    @pl.when(grp == 0)
+    def _():
+        rest_of_kt()
 
     def sweep(t, carry):
         par_in = (t + 1) % 2

time: 77 us -> 75.6 us (0.982)
  Pallas kernels: 71.9 us -> 70.5 us
    pallas_call x1, Pallas kernels: 71.9 us -> 70.5 us  [local_fn(): pl.pallas_call(lambda *refs: sinkhorn_kernel(n_chunk, norm, *refs), out_s...]
where the time goes in v2:
time: 75.6 us; the launch traced here: 75.5 us
  Pallas kernels  70.5 us (93%)
  local copies, waits for them, and re-layouts  4.36 us (6%)
    pallas_call x1, Pallas kernels, local_fn(): pl.pallas_call(lambda *refs: sinkhorn_kernel(n_chunk, norm, *refs), out_s...  70.5 us
    unnamed x3, local copies, waits for them, and re-layouts  4.36 us

profile of v2, /device:TPU:0, one launch (start us, length us, event | category | flops | bytes accessed | tf_op | source)
XLA Modules:
  0.0 75.5 jit_solution(16440872445739908178)
XLA Ops:
  0.6 70.5 %sinkhorn.1 = (f32[32,2048]{1,0:T(8,128)}, f32[32,1024]{1,0:T(8,128)}, f32[1,32]{1,0:T(1,128)}) custom-call(bf16[2048,1024]{1,0:T(8,128)(2,1)} %refs_0_.1, bf16[2048,1024]{1,0:T(8,128)(2,1)} %refs_1_.1, f32[32,2048]{1,0:T(8,128)} %bitcast.5, f32[32,1024]{1,0:T(8,128)} %bitcast.7), custom_call_target="tpu_custom_call" | custom-call | tf_op jit(solution)/shard_map/sinkhorn/pallas_call | solution.py:254
  71.1 1.7 %copy.10 = f32[2048,32]{0,1:T(8,128)} copy(f32[2048,32]{0,1:T(8,128)} %bitcast.6) | data formatting | bytes 524288
  72.8 1.6 %copy.11 = f32[1024,32]{0,1:T(8,128)} copy(f32[1024,32]{0,1:T(8,128)} %bitcast.8) | data formatting | bytes 262144
  74.4 1.1 %copy.12 = f32[32]{0:T(128)} copy(f32[32]{0:T(128)} %bitcast.9) | data formatting | bytes 256

commit v3 on v1

v3 whole, which is shorter than its diff:
```python
import jax
import jax.numpy as jnp
from jax import lax
from jax.experimental import pallas as pl
from jax.experimental.pallas import tpu as pltpu
from jax.sharding import PartitionSpec as P

SWEEPS = 6
F32 = jnp.float32
BF16 = jnp.bfloat16
MESH = pl.DeviceIdType.MESH


def sinkhorn_kernel(n_chunk, norm, k_hbm, c_hbm, a_hbm, b_hbm, u_hbm, v_hbm, cost_ref,
                    k_buf, kt_buf, c_buf, kct_buf, a_buf, b_buf, ub_buf, acc,
                    vb_buf, s_out, s_in, t_out, t_in, t0_buf, s0_buf, u_out, v_all, v_out, cost_part, cost_all,
                    k_sem, kp_send, kp_recv, c_sem, ab_sem, bp_sem, s0_send, s0_recv,
                    s_send, s_recv, t_send, t_recv, fin_sem, cs_send, cs_recv, out_sem,
                    kc_send, kc_recv, t0_send_sem, t0p_send, t0p_recv):
    rows, half = k_hbm.shape
    cols = 2 * half
    rw = rows // n_chunk
    cw = cols // n_chunk
    per_half = n_chunk // 2
    nq = b_buf.shape[1]
    row = lax.axis_index("row")
    col = lax.axis_index("col")
    prob = lax.axis_index("prob")
    x = col // 2
    core = col % 2
    grp = (core + x + row) % 2
    me = row * 4 + col
    mine = pl.ds(pl.multiple_of(grp * nq, nq), nq)
    other = pl.ds(pl.multiple_of((1 - grp) * nq, nq), nq)

    def dev(r, c):
        return (prob, r, c)

    partner = dev(row, 2 * x + 1 - core)
    x_peer = dev(row, 2 * (1 - x) + 1 - core)
    y_peer = dev(1 - row, 2 * x + 1 - core)

    def remote(src, dst, send, recv, to):
        return pltpu.make_async_remote_copy(src_ref=src, dst_ref=dst, send_sem=send, recv_sem=recv,
                                            device_id=to, device_id_type=MESH)

    def krows(i):
        return pl.ds(i * rw, rw)

    k_load = [pltpu.make_async_copy(k_hbm.at[krows(i)], k_buf.at[core, krows(i)], k_sem.at[i]) for i in range(n_chunk)]
    c_load = [pltpu.make_async_copy(c_hbm.at[krows(i)], c_buf.at[krows(i)], c_sem.at[i]) for i in range(n_chunk)]
    a_load = pltpu.make_async_copy(a_hbm, a_buf, ab_sem.at[0])
    b_load = pltpu.make_async_copy(b_hbm.at[mine], b_buf.at[core], ab_sem.at[1])
    for d in k_load:
        d.start()
    a_load.start()
    b_load.start()

    barrier = pltpu.get_barrier_semaphore()
    for dr in range(2):
        for dc in range(4):
            if dr or dc:
                pl.semaphore_signal(barrier, inc=1, device_id=dev((row + dr) % 2, (col + dc) % 4), device_id_type=MESH)

    blk = 256

    def transpose_rows(h, i):
        def body(n, carry):
            jo = pl.multiple_of(n * blk, blk)
            for ii in range(rw // blk):
                kt_buf[pl.ds(pl.multiple_of(h * half + jo, blk), blk), pl.ds(i * rw + ii * blk, blk)] = (
                    k_buf[h, pl.ds(i * rw + ii * blk, blk), pl.ds(jo, blk)].T)
            return carry
        lax.fori_loop(0, half // blk, body, 0)

    def kct_copy(i):
        part = kct_buf.at[pl.ds(pl.multiple_of(core * half, half), half), pl.ds(pl.multiple_of(i * rw, rw), rw)]
        return remote(part, part, kc_send.at[i], kc_recv.at[i], partner)

    def build_kct(i):
        pltpu.make_async_copy(c_hbm.at[pl.ds(i * rw, rw)], c_buf.at[pl.ds(i * rw, rw)], c_sem.at[i]).wait()
        def body(n, carry):
            jo = pl.multiple_of(n * blk, blk)
            for ii in range(rw // blk):
                rs = pl.ds(pl.multiple_of(i * rw + ii * blk, blk), blk)
                kct_buf[pl.ds(pl.multiple_of(core * half + jo, blk), blk), rs] = (
                    k_buf[core, rs, pl.ds(jo, blk)] * c_buf[rs, pl.ds(jo, blk)]).T
            return carry
        lax.fori_loop(0, half // blk, body, 0)
        kct_copy(i).start()

    k_push = [remote(k_buf.at[core, krows(i)], k_buf.at[core, krows(i)], kp_send.at[i], kp_recv.at[i], partner) for i in range(n_chunk)]
    b_push = remote(b_hbm.at[other], b_buf.at[core], bp_sem.at[0], bp_sem.at[1], partner)
    pl.semaphore_wait(barrier, 7)
    b_push.start()
    ones = jnp.ones((nq, half), BF16)
    for i in range(n_chunk):
        k_load[i].wait()
        if i == 0:
            k_push[0].start()
        part = lax.dot_general(ones, k_buf[core, krows(i)], (((1,), (1,)), ((), ())), preferred_element_type=F32)
        for n in range(rw // 128):
            r = i * (rw // 128) + n
            s0_buf[col, r:r + 1, :] = part[0:1, n * 128:(n + 1) * 128]
    s0_copies = []
    for n in range(1, 4):
        d = remote(s0_buf.at[col], s0_buf.at[col], s0_send.at[n], s0_recv.at[n], dev(row, (col + n) % 4))
        d.start()
        s0_copies.append(d)
    for i in range(1, n_chunk - 1):
        k_push[i].start()
    for d in c_load:
        d.start()
    for i in range(n_chunk):
        transpose_rows(core, i)
    a_load.wait()
    b_load.wait()
    for n in range(1, 4):
        frm = (col + 4 - n) % 4
        remote(s0_buf.at[frm], s0_buf.at[frm], s0_send.at[n], s0_recv.at[n], dev(row, frm)).wait_recv()
    s0 = (s0_buf[0] + s0_buf[1]) + (s0_buf[2] + s0_buf[3])
    for r in range(rows // 128):
        cs = slice(r * 128, (r + 1) * 128)
        ub_buf[:, cs] = (a_buf[:, cs] / s0[r:r + 1, :]).astype(BF16)

    def t_copy(par, o):
        return remote(t_out.at[o], t_in.at[par, o], t_send.at[o], t_recv.at[par, o], y_peer)

    def s_copy(par, o):
        return remote(s_out.at[o], s_in.at[par, o], s_send.at[o], s_recv.at[par, o], x_peer)

    t0_copies = []

    def t0_send(g, n):
        d = remote(t0_buf.at[g, n], t_in.at[0, core * per_half + n], t0_send_sem.at[g, n], t_recv.at[0, core * per_half + n],
                   dev(1 - row, 2 * x + (g + x + 1 - row) % 2))
        d.start()
        t0_copies.append(d)

    for n in range(per_half):
        part = jnp.dot(ub_buf[...], k_buf[core, :, n * cw:(n + 1) * cw], preferred_element_type=F32)
        for g in range(2):
            t0_buf[g, n] = part[g * nq:(g + 1) * nq]
        t0_send(0, n)
    for n in range(per_half):
        t0_send(1, n)
    for n in range(per_half):
        o = core * per_half + n
        d = remote(t0_buf.at[1 - grp, n], t_out.at[o], t0p_send.at[n], t0p_recv.at[n], partner)
        d.start()
        t0_copies.append(d)
        t_out[o] = t0_buf[grp, n]
    k_push[n_chunk - 1].start()

    def v_of(par, o):
        return b_buf[o // per_half, :, (o % per_half) * cw:(o % per_half + 1) * cw] / (t_out[o] + t_in[par, o])

    def first_v(h, n):
        o = h * per_half + n
        remote(t0_buf.at[0, n], t_in.at[0, o], t0_send_sem.at[0, n], t_recv.at[0, o], y_peer).wait_recv()
        return (b_buf[h, :, n * cw:(n + 1) * cw] / (t_out[o] + t_in[0, o])).astype(BF16)

    remote(b_hbm.at[other], b_buf.at[1 - core], bp_sem.at[0], bp_sem.at[1], partner).wait_recv()
    for n in range(per_half):
        prod = jnp.dot(first_v(core, n), kt_buf[pl.ds(pl.multiple_of(core * half + n * cw, cw), cw), :], preferred_element_type=F32)
        acc[...] = prod if n == 0 else acc[...] + prod
    for n in range(per_half):
        o = (1 - core) * per_half + n
        remote(t0_buf.at[0, n], t_out.at[o], t0p_send.at[n], t0p_recv.at[n], partner).wait_recv()
        vb_buf[:, n * cw:(n + 1) * cw] = first_v(1 - core, n)
    for o in range(n_chunk):
        remote(k_buf.at[1 - core, krows(o)], k_buf.at[1 - core, krows(o)], kp_send.at[o], kp_recv.at[o], partner).wait_recv()
        prod = lax.dot_general(vb_buf[...], k_buf[1 - core, krows(o)], (((1,), (1,)), ((), ())), preferred_element_type=F32)
        s_out[o] = acc[:, o * rw:(o + 1) * rw] + prod
        s_copy(1, o).start()
    for d in t0_copies:
        d.wait_send()
    for i in range(n_chunk):
        transpose_rows(1 - core, i)

    def u_and_t(par):
        for c in range(n_chunk):
            s_copy(par, c).wait()
            w = slice(c * rw, (c + 1) * rw)
            u = a_buf[mine, w] / (s_out[c] + s_in[par, c])
            u_out[mine, w] = u
            ub = u.astype(BF16)
            if c < n_chunk - 1:
                for h in range(2):
                    hc = slice(h * half, (h + 1) * half)
                    prod = jnp.dot(ub, k_buf[h, w, :], preferred_element_type=F32)
                    acc[:, hc] = prod if c == 0 else acc[:, hc] + prod
            else:
                for o in range(n_chunk):
                    oc = slice(o * cw, (o + 1) * cw)
                    hc = slice((o % per_half) * cw, (o % per_half + 1) * cw)
                    t_out[o] = acc[:, oc] + jnp.dot(ub, k_buf[o // per_half, w, hc], preferred_element_type=F32)
                    t_copy(par, o).start()

    def v_and_s(par_in, par):
        for c in range(n_chunk):
            t_copy(par_in, c).wait()
            vb = v_of(par_in, c).astype(BF16)
            w = slice(c * cw, (c + 1) * cw)
            if c < n_chunk - 1:
                prod = jnp.dot(vb, kt_buf[w, :], preferred_element_type=F32)
                acc[...] = prod if c == 0 else acc[...] + prod
            else:
                for o in range(n_chunk):
                    oc = slice(o * rw, (o + 1) * rw)
                    s_out[o] = acc[:, oc] + jnp.dot(vb, kt_buf[w, oc], preferred_element_type=F32)
                    s_copy(par, o).start()

    def sweep(t, carry):
        u_and_t(t % 2)
        build_kct(t - 1)
        v_and_s(t % 2, (t + 1) % 2)
        return carry

    lax.fori_loop(1, SWEEPS - 1, sweep, 0)
    last = (SWEEPS - 1) % 2
    u_and_t(last)

    u_push = remote(u_out.at[mine], u_out.at[mine], fin_sem.at[0], fin_sem.at[1], partner)
    u_push.start()
    cost_part[...] = jnp.zeros_like(cost_part)
    for d in s0_copies + k_push:
        d.wait_send()
    b_push.wait_send()
    for i in range(n_chunk):
        other_part = kct_buf.at[pl.ds(pl.multiple_of((1 - core) * half, half), half), krows(i)]
        remote(other_part, other_part, kc_send.at[i], kc_recv.at[i], partner).wait_recv()
        kct_copy(i).wait_send()
    for c in range(n_chunk):
        t_copy(last, c).wait()
        v = v_of(last, c)
        v_all[c // per_half, :, (c % per_half) * cw:(c % per_half + 1) * cw] = v
        prod = jnp.dot(v.astype(BF16), kct_buf[c * cw:(c + 1) * cw, :], preferred_element_type=F32)
        if c < n_chunk - 1:
            acc[...] = prod if c == 0 else acc[...] + prod
        else:
            w = (acc[...] + prod) * u_out[mine]
    v_push = remote(v_all.at[1 - core], v_out.at[mine], fin_sem.at[2], fin_sem.at[3], partner)
    v_push.start()
    tot = w[:, 0:128]
    for n in range(1, rows // 128):
        tot = tot + w[:, n * 128:(n + 1) * 128]
    cost_part[mine] = tot
    cost_all[me] = jnp.sum(cost_part[...].T, axis=0, keepdims=True)
    cost_copies = []
    for dr in range(2):
        for dc in range(4):
            if dr or dc:
                n = dr * 4 + dc
                d = remote(cost_all.at[me], cost_all.at[me], cs_send.at[n], cs_recv.at[n], dev((row + dr) % 2, (col + dc) % 4))
                d.start()
                cost_copies.append((n, (row + dr) % 2, (col + 4 - dc) % 4, d))
    v_out[mine] = v_all[core]
    remote(u_out.at[other], u_out.at[other], fin_sem.at[0], fin_sem.at[1], partner).wait_recv()
    u_push.wait_send()
    u_store = pltpu.make_async_copy(u_out, u_hbm, out_sem.at[0])
    u_store.start()
    remote(v_all.at[core], v_out.at[other], fin_sem.at[2], fin_sem.at[3], partner).wait_recv()
    v_push.wait_send()
    v_store = pltpu.make_async_copy(v_out, v_hbm, out_sem.at[1])
    v_store.start()
    for n, fr, fc, d in cost_copies:
        f = fr * 4 + fc
        remote(cost_all.at[f], cost_all.at[f], cs_send.at[n], cs_recv.at[n], dev(fr, fc)).wait_recv()
    total = cost_all[0]
    for n in range(1, 8):
        total = total + cost_all[n]
    cost_ref[...] = total[:, :cost_ref.shape[1]] * norm
    for n, fr, fc, d in cost_copies:
        d.wait_send()
    u_store.wait()
    v_store.wait()


def solution(mesh):
    n_chunk = 4

    def local_fn(kernel, cost_mat, src_mass, tgt_mass):
        rows, half = kernel.shape
        nprob = src_mass.shape[1]
        nq = nprob // 2
        cols = 2 * half
        rw, cw = rows // n_chunk, cols // n_chunk
        norm = 1.0 / float(rows * mesh.shape["row"] * half * mesh.shape["col"])
        any_spec = pl.BlockSpec(memory_space=pl.ANY)
        dma = pltpu.SemaphoreType.DMA
        u_t, v_t, cost = pl.pallas_call(
            lambda *refs: sinkhorn_kernel(n_chunk, norm, *refs),
            out_shape=(jax.ShapeDtypeStruct((nprob, rows), F32), jax.ShapeDtypeStruct((nprob, half), F32),
                       jax.ShapeDtypeStruct((1, nprob), F32)),
            in_specs=[any_spec] * 4,
            out_specs=(any_spec, any_spec, pl.BlockSpec(memory_space=pltpu.VMEM)),
            scratch_shapes=[
                pltpu.VMEM((2, rows, half), BF16),
                pltpu.VMEM((cols, rows), BF16),
                pltpu.VMEM((rows, half), BF16),
                pltpu.VMEM((cols, rows), BF16),
                pltpu.VMEM((nprob, rows), F32),
                pltpu.VMEM((2, nq, half), F32),
                pltpu.VMEM((nprob, rows), BF16),
                pltpu.VMEM((nq, max(rows, cols)), F32),
                pltpu.VMEM((nq, half), BF16),
                pltpu.VMEM((n_chunk, nq, rw), F32),
                pltpu.VMEM((2, n_chunk, nq, rw), F32),
                pltpu.VMEM((n_chunk, nq, cw), F32),
                pltpu.VMEM((2, n_chunk, nq, cw), F32),
                pltpu.VMEM((2, n_chunk // 2, nq, cw), F32),
                pltpu.VMEM((4, rows // 128, 128), F32),
                pltpu.VMEM((nprob, rows), F32),
                pltpu.VMEM((2, nq, half), F32),
                pltpu.VMEM((nprob, half), F32),
                pltpu.VMEM((128, 128), F32),
                pltpu.VMEM((8, 1, 128), F32),
                dma((n_chunk,)), dma((n_chunk,)), dma((n_chunk,)), dma((n_chunk,)), dma((2,)), dma((2,)), dma((4,)), dma((4,)),
                dma((n_chunk,)), dma((2, n_chunk)), dma((n_chunk,)), dma((2, n_chunk)), dma((4,)), dma((8,)), dma((8,)), dma((2,)),
                dma((n_chunk,)), dma((n_chunk,)), dma((2, n_chunk // 2)), dma((n_chunk // 2,)), dma((n_chunk // 2,)),
            ],
            compiler_params=pltpu.CompilerParams(collective_id=0, has_side_effects=True, vmem_limit_bytes=60 * 1024 * 1024),
            name="sinkhorn",
        )(kernel, cost_mat, src_mass.T, tgt_mass.T)
        return u_t.T, v_t.T, cost.reshape(nprob)

    return jax.shard_map(local_fn, mesh=mesh, in_specs=(P("row", "col"), P("row", "col"), P("row", "prob"), P("col", "prob")), out_specs=(P("row", "prob"), P("col", "prob"), P("prob")), check_vma=False)
```

time: 77 us -> 71.5 us (0.929)
  Pallas kernels: 71.9 us -> 66.4 us
    pallas_call x1, Pallas kernels: 71.9 us -> 66.4 us  [local_fn(): pl.pallas_call(lambda *refs: sinkhorn_kernel(n_chunk, norm, *refs), out_s...]
where the time goes in v3:
time: 71.5 us; the launch traced here: 71.4 us
  Pallas kernels  66.4 us (93%)
  local copies, waits for them, and re-layouts  4.36 us (6%)
    pallas_call x1, Pallas kernels, local_fn(): pl.pallas_call(lambda *refs: sinkhorn_kernel(n_chunk, norm, *refs), out_s...  66.4 us
    unnamed x3, local copies, waits for them, and re-layouts  4.36 us

profile of v3, /device:TPU:0, one launch (start us, length us, event | category | flops | bytes accessed | tf_op | source)
XLA Modules:
  0.0 71.4 jit_solution(6220100442744736042)
XLA Ops:
  0.6 66.4 %sinkhorn.1 = (f32[32,2048]{1,0:T(8,128)}, f32[32,1024]{1,0:T(8,128)}, f32[1,32]{1,0:T(1,128)}) custom-call(bf16[2048,1024]{1,0:T(8,128)(2,1)} %refs_0_.1, bf16[2048,1024]{1,0:T(8,128)(2,1)} %refs_1_.1, f32[32,2048]{1,0:T(8,128)} %bitcast.5, f32[32,1024]{1,0:T(8,128)} %bitcast.7), custom_call_target="tpu_custom_call" | custom-call | tf_op jit(solution)/shard_map/sinkhorn/pallas_call | solution.py:292
  67.0 1.7 %copy.10 = f32[2048,32]{0,1:T(8,128)} copy(f32[2048,32]{0,1:T(8,128)} %bitcast.6) | data formatting | bytes 524288
  68.7 1.6 %copy.11 = f32[1024,32]{0,1:T(8,128)} copy(f32[1024,32]{0,1:T(8,128)} %bitcast.8) | data formatting | bytes 262144
  70.2 1.1 %copy.12 = f32[32]{0:T(128)} copy(f32[32]{0:T(128)} %bitcast.9) | data formatting | bytes 256

commit v4 on v3

--- a/solution.py
+++ b/solution.py
@@ -13,7 +13,7 @@
 
 def sinkhorn_kernel(n_chunk, norm, k_hbm, c_hbm, a_hbm, b_hbm, u_hbm, v_hbm, cost_ref,
                     k_buf, kt_buf, c_buf, kct_buf, a_buf, b_buf, ub_buf, acc,
-                    vb_buf, s_out, s_in, t_out, t_in, t0_buf, s0_buf, u_out, v_all, v_out, cost_part, cost_all,
+                    s_out, s_in, t_out, t_in, t0_buf, s0_buf, u_out, v_all, v_out, cost_part, cost_all,
                     k_sem, kp_send, kp_recv, c_sem, ab_sem, bp_sem, s0_send, s0_recv,
                     s_send, s_recv, t_send, t_recv, fin_sem, cs_send, cs_recv, out_sem,
                     kc_send, kc_recv, t0_send_sem, t0p_send, t0p_recv):
@@ -161,22 +161,31 @@
         return (b_buf[h, :, n * cw:(n + 1) * cw] / (t_out[o] + t_in[0, o])).astype(BF16)
 
     remote(b_hbm.at[other], b_buf.at[1 - core], bp_sem.at[0], bp_sem.at[1], partner).wait_recv()
-    for n in range(per_half):
-        prod = jnp.dot(first_v(core, n), kt_buf[pl.ds(pl.multiple_of(core * half + n * cw, cw), cw), :], preferred_element_type=F32)
-        acc[...] = prod if n == 0 else acc[...] + prod
-    for n in range(per_half):
-        o = (1 - core) * per_half + n
-        remote(t0_buf.at[0, n], t_out.at[o], t0p_send.at[n], t0p_recv.at[n], partner).wait_recv()
-        vb_buf[:, n * cw:(n + 1) * cw] = first_v(1 - core, n)
-    for o in range(n_chunk):
-        remote(k_buf.at[1 - core, krows(o)], k_buf.at[1 - core, krows(o)], kp_send.at[o], kp_recv.at[o], partner).wait_recv()
-        prod = lax.dot_general(vb_buf[...], k_buf[1 - core, krows(o)], (((1,), (1,)), ((), ())), preferred_element_type=F32)
-        s_out[o] = acc[:, o * rw:(o + 1) * rw] + prod
-        s_copy(1, o).start()
+    for i in range(n_chunk):
+        remote(k_buf.at[1 - core, krows(i)], k_buf.at[1 - core, krows(i)], kp_send.at[i], kp_recv.at[i], partner).wait_recv()
+        transpose_rows(1 - core, i)
+
+    @pl.when(grp == 1)
+    def _():
+        for i in range(n_chunk):
+            build_kct(i)
+
+    for m in range(n_chunk):
+        h = core if m < per_half else 1 - core
+        n = m % per_half
+        if m >= per_half:
+            remote(t0_buf.at[0, n], t_out.at[h * per_half + n], t0p_send.at[n], t0p_recv.at[n], partner).wait_recv()
+        vb = first_v(h, n)
+        js = pl.ds(pl.multiple_of(h * half + n * cw, cw), cw)
+        if m < n_chunk - 1:
+            prod = jnp.dot(vb, kt_buf[js, :], preferred_element_type=F32)
+            acc[...] = prod if m == 0 else acc[...] + prod
+        else:
+            for o in range(n_chunk):
+                s_out[o] = acc[:, o * rw:(o + 1) * rw] + jnp.dot(vb, kt_buf[js, o * rw:(o + 1) * rw], preferred_element_type=F32)
+                s_copy(1, o).start()
     for d in t0_copies:
         d.wait_send()
-    for i in range(n_chunk):
-        transpose_rows(1 - core, i)
 
     def u_and_t(par):
         for c in range(n_chunk):
@@ -213,7 +222,11 @@
 
     def sweep(t, carry):
         u_and_t(t % 2)
-        build_kct(t - 1)
+
+        @pl.when(grp == 0)
+        def _():
+            build_kct(t - 1)
+
         v_and_s(t % 2, (t + 1) % 2)
         return carry
 
@@ -304,7 +317,6 @@
                 pltpu.VMEM((2, nq, half), F32),
                 pltpu.VMEM((nprob, rows), BF16),
                 pltpu.VMEM((nq, max(rows, cols)), F32),
-                pltpu.VMEM((nq, half), BF16),
                 pltpu.VMEM((n_chunk, nq, rw), F32),
                 pltpu.VMEM((2, n_chunk, nq, rw), F32),
                 pltpu.VMEM((n_chunk, nq, cw), F32),

time: 71.5 us -> 64.2 us (0.90)
  Pallas kernels: 66.4 us -> 59 us
    pallas_call x1, Pallas kernels: 66.4 us -> 59 us  [local_fn(): pl.pallas_call(lambda *refs: sinkhorn_kernel(n_chunk, norm, *refs), out_s...]
where the time goes in v4:
time: 64.2 us; the launch traced here: 64 us
  Pallas kernels  59 us (92%)
  local copies, waits for them, and re-layouts  4.36 us (7%)
    pallas_call x1, Pallas kernels, local_fn(): pl.pallas_call(lambda *refs: sinkhorn_kernel(n_chunk, norm, *refs), out_s...  59 us
    unnamed x3, local copies, waits for them, and re-layouts  4.36 us

profile of v4, /device:TPU:0, one launch (start us, length us, event | category | flops | bytes accessed | tf_op | source)
XLA Modules:
  0.0 64.0 jit_solution(17223702132005372170)
XLA Ops:
  0.6 59.0 %sinkhorn.1 = (f32[32,2048]{1,0:T(8,128)}, f32[32,1024]{1,0:T(8,128)}, f32[1,32]{1,0:T(1,128)}) custom-call(bf16[2048,1024]{1,0:T(8,128)(2,1)} %refs_0_.1, bf16[2048,1024]{1,0:T(8,128)(2,1)} %refs_1_.1, f32[32,2048]{1,0:T(8,128)} %bitcast.5, f32[32,1024]{1,0:T(8,128)} %bitcast.7), custom_call_target="tpu_custom_call" | custom-call | tf_op jit(solution)/shard_map/sinkhorn/pallas_call | solution.py:305
  59.7 1.7 %copy.10 = f32[2048,32]{0,1:T(8,128)} copy(f32[2048,32]{0,1:T(8,128)} %bitcast.6) | data formatting | bytes 524288
  61.4 1.6 %copy.11 = f32[1024,32]{0,1:T(8,128)} copy(f32[1024,32]{0,1:T(8,128)} %bitcast.8) | data formatting | bytes 262144
  62.9 1.1 %copy.12 = f32[32]{0:T(128)} copy(f32[32]{0:T(128)} %bitcast.9) | data formatting | bytes 256

commit v5 on v4

--- a/solution.py
+++ b/solution.py
@@ -11,11 +11,11 @@
 MESH = pl.DeviceIdType.MESH
 
 
-def sinkhorn_kernel(n_chunk, norm, k_hbm, c_hbm, a_hbm, b_hbm, u_hbm, v_hbm, cost_ref,
+def sinkhorn_kernel(n_chunk, k_hbm, c_hbm, a_hbm, b_hbm, u_out, v_out, cost_all,
                     k_buf, kt_buf, c_buf, kct_buf, a_buf, b_buf, ub_buf, acc,
-                    s_out, s_in, t_out, t_in, t0_buf, s0_buf, u_out, v_all, v_out, cost_part, cost_all,
+                    s_out, s_in, t_out, t_in, t0_buf, s0_buf, v_all, cost_part,
                     k_sem, kp_send, kp_recv, c_sem, ab_sem, bp_sem, s0_send, s0_recv,
-                    s_send, s_recv, t_send, t_recv, fin_sem, cs_send, cs_recv, out_sem,
+                    s_send, s_recv, t_send, t_recv, fin_sem, cs_send, cs_recv,
                     kc_send, kc_recv, t0_send_sem, t0p_send, t0p_recv):
     rows, half = k_hbm.shape
     cols = 2 * half
@@ -271,23 +271,25 @@
     v_out[mine] = v_all[core]
     remote(u_out.at[other], u_out.at[other], fin_sem.at[0], fin_sem.at[1], partner).wait_recv()
     u_push.wait_send()
-    u_store = pltpu.make_async_copy(u_out, u_hbm, out_sem.at[0])
-    u_store.start()
     remote(v_all.at[core], v_out.at[other], fin_sem.at[2], fin_sem.at[3], partner).wait_recv()
     v_push.wait_send()
-    v_store = pltpu.make_async_copy(v_out, v_hbm, out_sem.at[1])
-    v_store.start()
     for n, fr, fc, d in cost_copies:
         f = fr * 4 + fc
         remote(cost_all.at[f], cost_all.at[f], cs_send.at[n], cs_recv.at[n], dev(fr, fc)).wait_recv()
-    total = cost_all[0]
-    for n in range(1, 8):
-        total = total + cost_all[n]
-    cost_ref[...] = total[:, :cost_ref.shape[1]] * norm
     for n, fr, fc, d in cost_copies:
         d.wait_send()
-    u_store.wait()
-    v_store.wait()
+
+
+def output_kernel(norm, u_ref, v_ref, c_ref, u_hbm, v_hbm, cost_ref, sem):
+    stores = [pltpu.make_async_copy(u_ref, u_hbm, sem.at[0]), pltpu.make_async_copy(v_ref, v_hbm, sem.at[1])]
+    for d in stores:
+        d.start()
+    total = c_ref[0]
+    for n in range(1, 8):
+        total = total + c_ref[n]
+    cost_ref[...] = total[:, :cost_ref.shape[1]] * norm
+    for d in stores:
+        d.wait()
 
 
 def solution(mesh):
@@ -300,14 +302,14 @@
         cols = 2 * half
         rw, cw = rows // n_chunk, cols // n_chunk
         norm = 1.0 / float(rows * mesh.shape["row"] * half * mesh.shape["col"])
+        vmem_spec = pl.BlockSpec(memory_space=pltpu.VMEM)
         any_spec = pl.BlockSpec(memory_space=pl.ANY)
         dma = pltpu.SemaphoreType.DMA
-        u_t, v_t, cost = pl.pallas_call(
-            lambda *refs: sinkhorn_kernel(n_chunk, norm, *refs),
-            out_shape=(jax.ShapeDtypeStruct((nprob, rows), F32), jax.ShapeDtypeStruct((nprob, half), F32),
-                       jax.ShapeDtypeStruct((1, nprob), F32)),
+        u_vm, v_vm, c_vm = pl.pallas_call(
+            lambda *refs: sinkhorn_kernel(n_chunk, *refs),
+            out_shape=(pltpu.VMEM((nprob, rows), F32), pltpu.VMEM((nprob, half), F32), pltpu.VMEM((8, 1, 128), F32)),
             in_specs=[any_spec] * 4,
-            out_specs=(any_spec, any_spec, pl.BlockSpec(memory_space=pltpu.VMEM)),
+            out_specs=(vmem_spec, vmem_spec, vmem_spec),
             scratch_shapes=[
                 pltpu.VMEM((2, rows, half), BF16),
                 pltpu.VMEM((cols, rows), BF16),
@@ -323,18 +325,24 @@
                 pltpu.VMEM((2, n_chunk, nq, cw), F32),
                 pltpu.VMEM((2, n_chunk // 2, nq, cw), F32),
                 pltpu.VMEM((4, rows // 128, 128), F32),
-                pltpu.VMEM((nprob, rows), F32),
                 pltpu.VMEM((2, nq, half), F32),
-                pltpu.VMEM((nprob, half), F32),
                 pltpu.VMEM((128, 128), F32),
-                pltpu.VMEM((8, 1, 128), F32),
                 dma((n_chunk,)), dma((n_chunk,)), dma((n_chunk,)), dma((n_chunk,)), dma((2,)), dma((2,)), dma((4,)), dma((4,)),
-                dma((n_chunk,)), dma((2, n_chunk)), dma((n_chunk,)), dma((2, n_chunk)), dma((4,)), dma((8,)), dma((8,)), dma((2,)),
+                dma((n_chunk,)), dma((2, n_chunk)), dma((n_chunk,)), dma((2, n_chunk)), dma((4,)), dma((8,)), dma((8,)),
                 dma((n_chunk,)), dma((n_chunk,)), dma((2, n_chunk // 2)), dma((n_chunk // 2,)), dma((n_chunk // 2,)),
             ],
             compiler_params=pltpu.CompilerParams(collective_id=0, has_side_effects=True, vmem_limit_bytes=60 * 1024 * 1024),
             name="sinkhorn",
         )(kernel, cost_mat, src_mass.T, tgt_mass.T)
+        u_t, v_t, cost = pl.pallas_call(
+            lambda *refs: output_kernel(norm, *refs),
+            out_shape=(jax.ShapeDtypeStruct((nprob, rows), F32), jax.ShapeDtypeStruct((nprob, half), F32),
+                       jax.ShapeDtypeStruct((1, nprob), F32)),
+            in_specs=[vmem_spec] * 3,
+            out_specs=(any_spec, any_spec, vmem_spec),
+            scratch_shapes=[dma((2,))],
+            name="outputs",
+        )(*(pltpu.with_memory_space_constraint(r, pltpu.VMEM) for r in (u_vm, v_vm, c_vm)))
         return u_t.T, v_t.T, cost.reshape(nprob)
 
     return jax.shard_map(local_fn, mesh=mesh, in_specs=(P("row", "col"), P("row", "col"), P("row", "prob"), P("col", "prob")), out_specs=(P("row", "prob"), P("col", "prob"), P("prob")), check_vma=False)

time: 64.2 us -> 60.5 us (0.942)
  local copies, waits for them, and re-layouts: 4.36 us -> 0 us
  Pallas kernels: 59 us -> 59.8 us
    unnamed x3 -> x0, local copies, waits for them, and re-layouts: 4.36 us -> none
    pallas_call x1 -> x2, Pallas kernels: 59 us -> 59.8 us  [the longest x1 58.5 us: local_fn(): pl.pallas_call(lambda *refs: sinkhorn_kernel(n_chunk, *refs), out_shape=(...]
where the time goes in v5:
time: 60.5 us; the launch traced here: 60.4 us
  Pallas kernels  59.8 us (99%)
  between operations  0.64 us (1%)
    pallas_call x1, Pallas kernels, local_fn(): pl.pallas_call(lambda *refs: sinkhorn_kernel(n_chunk, *refs), out_shape=(...  58.5 us
    pallas_call x1, Pallas kernels, local_fn(): pl.pallas_call(lambda *refs: output_kernel(norm, *refs), out_shape=(jax.S...  1.27 us

profile of v5, /device:TPU:0, one launch (start us, length us, event | category | flops | bytes accessed | tf_op | source)
XLA Modules:
  0.0 60.4 jit_solution(3292125994265162535)
XLA Ops:
  0.6 58.5 %sinkhorn.1 = (f32[32,2048]{1,0:T(8,128)S(1)}, f32[32,1024]{1,0:T(8,128)S(1)}, f32[8,1,128]{2,1,0:T(1,128)S(1)}) custom-call(bf16[2048,1024]{1,0:T(8,128)(2,1)} %refs_0_.1, bf16[2048,1024]{1,0:T(8,128)(2,1)} %refs_1_.1, f32[32,2048]{1,0:T(8,128)} %bitcast.5, f32[32,1024]{1,0:T(8,128)} %bitcast.6), custom_call_target="tpu_custom_call" | custom-call | tf_op jit(solution)/shard_map/sinkhorn/pallas_call | solution.py:308
  59.1 1.3 %outputs.1 = (f32[32,2048]{1,0:T(8,128)}, f32[32,1024]{1,0:T(8,128)}, f32[1,32]{1,0:T(1,128)}) custom-call(f32[32,2048]{1,0:T(8,128)S(1)} %get-tuple-element.9.refs_0_, f32[32,1024]{1,0:T(8,128)S(1)} %get-tuple-element.10.refs_1_, f32[8,1,128]{2,1,0:T(1,128)S(1)} %get-tuple-element.11.refs_2_), custom_call_target="tpu_custom_call" | custom-call | tf_op jit(solution)/shard_map/outputs/pallas_call | solution.py:337

commit v6 on v5

v6 whole, which is shorter than its diff:
```python
import jax
import jax.numpy as jnp
from jax import lax
from jax.experimental import pallas as pl
from jax.experimental.pallas import tpu as pltpu
from jax.sharding import PartitionSpec as P

SWEEPS = 6
F32 = jnp.float32
BF16 = jnp.bfloat16
MESH = pl.DeviceIdType.MESH


def sinkhorn_kernel(n_chunk, k_hbm, c_hbm, a_hbm, b_hbm, u_out, v_out, cost_all,
                    k_buf, kt_buf, c_buf, kct_buf, a_buf, b_buf, ub_buf, acc,
                    s_out, s_in, t_out, t_in, t0_buf, s0_buf, v_all, cost_part,
                    load_sem, send_sem, kp_recv, s_recv, t_recv, one_recv):
    rows, half = k_hbm.shape
    cols = 2 * half
    rw = rows // n_chunk
    cw = cols // n_chunk
    per_half = n_chunk // 2
    nq = b_buf.shape[1]
    row = lax.axis_index("row")
    col = lax.axis_index("col")
    prob = lax.axis_index("prob")
    x = col // 2
    core = col % 2
    grp = (core + x + row) % 2
    me = row * 4 + col
    mine = pl.ds(pl.multiple_of(grp * nq, nq), nq)
    other = pl.ds(pl.multiple_of((1 - grp) * nq, nq), nq)

    def dev(r, c):
        return (prob, r, c)

    partner = dev(row, 2 * x + 1 - core)
    x_peer = dev(row, 2 * (1 - x) + 1 - core)
    y_peer = dev(1 - row, 2 * x + 1 - core)

    def remote(src, dst, send, recv, to):
        return pltpu.make_async_remote_copy(src_ref=src, dst_ref=dst, send_sem=send, recv_sem=recv,
                                            device_id=to, device_id_type=MESH)

    KP, BP, S0, SS, TT, T0, TP, KC, US, VS, CS = range(11)

    def all_sent(ref, kind):
        remote(ref, ref, send_sem.at[kind], one_recv.at[0], partner).wait_send()

    def all_here(ref, recv):
        remote(ref, ref, send_sem.at[0], recv, partner).wait_recv()

    def krows(i):
        return pl.ds(i * rw, rw)

    k_load = [pltpu.make_async_copy(k_hbm.at[krows(i)], k_buf.at[core, krows(i)], load_sem.at[i]) for i in range(n_chunk)]
    c_load = [pltpu.make_async_copy(c_hbm.at[krows(i)], c_buf.at[krows(i)], load_sem.at[i]) for i in range(n_chunk)]
    a_load = pltpu.make_async_copy(a_hbm, a_buf, load_sem.at[n_chunk])
    b_load = pltpu.make_async_copy(b_hbm.at[mine], b_buf.at[core], load_sem.at[n_chunk + 1])
    for d in k_load:
        d.start()
    a_load.start()
    b_load.start()

    barrier = pltpu.get_barrier_semaphore()
    for dr in range(2):
        for dc in range(4):
            if dr or dc:
                pl.semaphore_signal(barrier, inc=1, device_id=dev((row + dr) % 2, (col + dc) % 4), device_id_type=MESH)

    blk = 256

    def transpose_rows(h, i):
        def body(n, carry):
            jo = pl.multiple_of(n * blk, blk)
            for ii in range(rw // blk):
                kt_buf[pl.ds(pl.multiple_of(h * half + jo, blk), blk), pl.ds(i * rw + ii * blk, blk)] = (
                    k_buf[h, pl.ds(i * rw + ii * blk, blk), pl.ds(jo, blk)].T)
            return carry
        lax.fori_loop(0, half // blk, body, 0)

    def kct_copy(i):
        part = kct_buf.at[pl.ds(pl.multiple_of(core * half, half), half), pl.ds(pl.multiple_of(i * rw, rw), rw)]
        return remote(part, part, send_sem.at[KC], one_recv.at[5], partner)

    def build_kct(i):
        pltpu.make_async_copy(c_hbm.at[pl.ds(i * rw, rw)], c_buf.at[pl.ds(i * rw, rw)], load_sem.at[i]).wait()
        def body(n, carry):
            jo = pl.multiple_of(n * blk, blk)
            for ii in range(rw // blk):
                rs = pl.ds(pl.multiple_of(i * rw + ii * blk, blk), blk)
                kct_buf[pl.ds(pl.multiple_of(core * half + jo, blk), blk), rs] = (
                    k_buf[core, rs, pl.ds(jo, blk)] * c_buf[rs, pl.ds(jo, blk)]).T
            return carry
        lax.fori_loop(0, half // blk, body, 0)
        kct_copy(i).start()

    k_push = [remote(k_buf.at[core, krows(i)], k_buf.at[core, krows(i)], send_sem.at[KP], kp_recv.at[i], partner) for i in range(n_chunk)]
    b_push = remote(b_hbm.at[other], b_buf.at[core], send_sem.at[BP], one_recv.at[0], partner)
    pl.semaphore_wait(barrier, 7)
    b_push.start()
    ones = jnp.ones((nq, half), BF16)
    for i in range(n_chunk):
        k_load[i].wait()
        if i == 0:
            k_push[0].start()
        if i % 2:
            part = lax.dot_general(ones, k_buf[core, pl.ds((i - 1) * rw, 2 * rw)], (((1,), (1,)), ((), ())), preferred_element_type=F32)
            for n in range(2 * rw // 128):
                r = (i - 1) * (rw // 128) + n
                s0_buf[col, r:r + 1, :] = part[0:1, n * 128:(n + 1) * 128]
    for n in range(1, 4):
        remote(s0_buf.at[col], s0_buf.at[col], send_sem.at[S0], one_recv.at[1], dev(row, (col + n) % 4)).start()
    for i in range(1, n_chunk):
        k_push[i].start()
    for d in c_load:
        d.start()
    for i in range(n_chunk):
        transpose_rows(core, i)
    a_load.wait()
    b_load.wait()
    all_here(s0_buf.at[0:3], one_recv.at[1])
    s0 = (s0_buf[0] + s0_buf[1]) + (s0_buf[2] + s0_buf[3])
    for r in range(rows // 128):
        cs = slice(r * 128, (r + 1) * 128)
        ub_buf[:, cs] = (a_buf[:, cs] / s0[r:r + 1, :]).astype(BF16)

    def t_copy(par, o):
        return remote(t_out.at[o], t_in.at[par, o], send_sem.at[TT], t_recv.at[par, o], y_peer)

    def s_copy(par, o):
        return remote(s_out.at[o], s_in.at[par, o], send_sem.at[SS], s_recv.at[par, o], x_peer)

    def t0_send(g, n):
        remote(t0_buf.at[g, n], t_in.at[0, core * per_half + n], send_sem.at[T0], t_recv.at[0, core * per_half + n],
               dev(1 - row, 2 * x + (g + x + 1 - row) % 2)).start()

    for n in range(per_half):
        part = jnp.dot(ub_buf[...], k_buf[core, :, n * cw:(n + 1) * cw], preferred_element_type=F32)
        for g in range(2):
            t0_buf[g, n] = part[g * nq:(g + 1) * nq]
        t0_send(0, n)
    for n in range(per_half):
        t0_send(1, n)
    for n in range(per_half):
        o = core * per_half + n
        remote(t0_buf.at[1 - grp, n], t_out.at[o], send_sem.at[TP], one_recv.at[2], partner).start()
        t_out[o] = t0_buf[grp, n]

    def v_of(par, o):
        return b_buf[o // per_half, :, (o % per_half) * cw:(o % per_half + 1) * cw] / (t_out[o] + t_in[par, o])

    all_here(b_buf.at[0], one_recv.at[0])
    for i in range(n_chunk):
        all_here(k_buf.at[1 - core, krows(i)], kp_recv.at[i])
        transpose_rows(1 - core, i)

    @pl.when(grp == 1)
    def _():
        for i in range(n_chunk):
            build_kct(i)

    all_here(t0_buf.at[0], one_recv.at[2])
    order = list(range(per_half, n_chunk)) + list(range(per_half))
    for c in order:
        all_here(t_in.at[0, c], t_recv.at[0, c])
        vb = v_of(0, c).astype(BF16)
        js = slice(c * cw, (c + 1) * cw)
        if c != order[-1]:
            prod = jnp.dot(vb, kt_buf[js, :], preferred_element_type=F32)
            acc[...] = prod if c == order[0] else acc[...] + prod
        else:
            for o in range(n_chunk):
                s_out[o] = acc[:, o * rw:(o + 1) * rw] + jnp.dot(vb, kt_buf[js, o * rw:(o + 1) * rw], preferred_element_type=F32)
                s_copy(1, o).start()
    all_sent(t0_buf, T0)
    all_sent(t0_buf.at[0], TP)
    all_sent(s0_buf.at[0:3], S0)
    all_sent(k_buf.at[0], KP)
    all_sent(b_buf.at[0], BP)

    @pl.when(grp == 0)
    def _():
        for i in range(n_chunk - 1):
            build_kct(i)

    def u_and_t(par):
        for c in range(n_chunk):
            all_here(s_in.at[par, c], s_recv.at[par, c])
            w = slice(c * rw, (c + 1) * rw)
            u = a_buf[mine, w] / (s_out[c] + s_in[par, c])
            u_out[mine, w] = u
            ub = u.astype(BF16)
            if c < n_chunk - 1:
                for h in range(2):
                    hc = slice(h * half, (h + 1) * half)
                    prod = jnp.dot(ub, k_buf[h, w, :], preferred_element_type=F32)
                    acc[:, hc] = prod if c == 0 else acc[:, hc] + prod
            else:
                all_sent(s_out, SS)
                for o in range(n_chunk):
                    oc = slice(o * cw, (o + 1) * cw)
                    hc = slice((o % per_half) * cw, (o % per_half + 1) * cw)
                    t_out[o] = acc[:, oc] + jnp.dot(ub, k_buf[o // per_half, w, hc], preferred_element_type=F32)
                    t_copy(par, o).start()

    def v_and_s(par_in, par):
        for c in range(n_chunk):
            all_here(t_in.at[par_in, c], t_recv.at[par_in, c])
            vb = v_of(par_in, c).astype(BF16)
            w = slice(c * cw, (c + 1) * cw)
            if c < n_chunk - 1:
                prod = jnp.dot(vb, kt_buf[w, :], preferred_element_type=F32)
                acc[...] = prod if c == 0 else acc[...] + prod
            else:
                all_sent(t_out, TT)
                for o in range(n_chunk):
                    oc = slice(o * rw, (o + 1) * rw)
                    s_out[o] = acc[:, oc] + jnp.dot(vb, kt_buf[w, oc], preferred_element_type=F32)
                    s_copy(par, o).start()

    def sweep(t, carry):
        u_and_t(t % 2)

        @pl.when((grp == 0) & (t == 1))
        def _():
            build_kct(n_chunk - 1)

        v_and_s(t % 2, (t + 1) % 2)
        return carry

    lax.fori_loop(1, SWEEPS - 1, sweep, 0)
    last = (SWEEPS - 1) % 2
    u_and_t(last)

    u_push = remote(u_out.at[mine], u_out.at[mine], send_sem.at[US], one_recv.at[3], partner)
    u_push.start()
    cost_part[...] = jnp.zeros_like(cost_part)
    all_here(kct_buf.at[0:half], one_recv.at[5])
    all_sent(kct_buf.at[0:half], KC)
    for c in range(n_chunk):
        all_here(t_in.at[last, c], t_recv.at[last, c])
        v = v_of(last, c)
        v_all[c // per_half, :, (c % per_half) * cw:(c % per_half + 1) * cw] = v
        prod = jnp.dot(v.astype(BF16), kct_buf[c * cw:(c + 1) * cw, :], preferred_element_type=F32)
        if c < n_chunk - 1:
            acc[...] = prod if c == 0 else acc[...] + prod
        else:
            w = (acc[...] + prod) * u_out[mine]
    v_push = remote(v_all.at[1 - core], v_out.at[mine], send_sem.at[VS], one_recv.at[4], partner)
    v_push.start()
    tot = w[:, 0:128]
    for n in range(1, rows // 128):
        tot = tot + w[:, n * 128:(n + 1) * 128]
    cost_part[mine] = tot
    cost_all[me] = jnp.sum(cost_part[...].T, axis=0, keepdims=True)
    for dr in range(2):
        for dc in range(4):
            if dr or dc:
                remote(cost_all.at[me], cost_all.at[me], send_sem.at[CS], one_recv.at[6], dev((row + dr) % 2, (col + dc) % 4)).start()
    v_out[mine] = v_all[core]
    all_sent(t_out, TT)
    all_here(u_out.at[other], one_recv.at[3])
    u_push.wait_send()
    all_here(v_out.at[other], one_recv.at[4])
    v_push.wait_send()
    all_here(cost_all.at[0:7], one_recv.at[6])
    all_sent(cost_all.at[0:7], CS)


def output_kernel(norm, u_ref, v_ref, c_ref, u_hbm, v_hbm, cost_ref, sem):
    stores = [pltpu.make_async_copy(u_ref, u_hbm, sem.at[0]), pltpu.make_async_copy(v_ref, v_hbm, sem.at[1])]
    for d in stores:
        d.start()
    total = c_ref[0]
    for n in range(1, 8):
        total = total + c_ref[n]
    cost_ref[...] = total[:, :cost_ref.shape[1]] * norm
    for d in stores:
        d.wait()


def solution(mesh):
    n_chunk = 4

    def local_fn(kernel, cost_mat, src_mass, tgt_mass):
        rows, half = kernel.shape
        nprob = src_mass.shape[1]
        nq = nprob // 2
        cols = 2 * half
        rw, cw = rows // n_chunk, cols // n_chunk
        norm = 1.0 / float(rows * mesh.shape["row"] * half * mesh.shape["col"])
        vmem_spec = pl.BlockSpec(memory_space=pltpu.VMEM)
        any_spec = pl.BlockSpec(memory_space=pl.ANY)
        dma = pltpu.SemaphoreType.DMA
        u_vm, v_vm, c_vm = pl.pallas_call(
            lambda *refs: sinkhorn_kernel(n_chunk, *refs),
            out_shape=(pltpu.VMEM((nprob, rows), F32), pltpu.VMEM((nprob, half), F32), pltpu.VMEM((8, 1, 128), F32)),
            in_specs=[any_spec] * 4,
            out_specs=(vmem_spec, vmem_spec, vmem_spec),
            scratch_shapes=[
                pltpu.VMEM((2, rows, half), BF16),
                pltpu.VMEM((cols, rows), BF16),
                pltpu.VMEM((rows, half), BF16),
                pltpu.VMEM((cols, rows), BF16),
                pltpu.VMEM((nprob, rows), F32),
                pltpu.VMEM((2, nq, half), F32),
                pltpu.VMEM((nprob, rows), BF16),
                pltpu.VMEM((nq, max(rows, cols)), F32),
                pltpu.VMEM((n_chunk, nq, rw), F32),
                pltpu.VMEM((2, n_chunk, nq, rw), F32),
                pltpu.VMEM((n_chunk, nq, cw), F32),
                pltpu.VMEM((2, n_chunk, nq, cw), F32),
                pltpu.VMEM((2, n_chunk // 2, nq, cw), F32),
                pltpu.VMEM((4, rows // 128, 128), F32),
                pltpu.VMEM((2, nq, half), F32),
                pltpu.VMEM((128, 128), F32),
                dma((n_chunk + 2,)), dma((11,)), dma((n_chunk,)), dma((2, n_chunk)), dma((2, n_chunk)), dma((7,)),
            ],
            compiler_params=pltpu.CompilerParams(collective_id=0, has_side_effects=True, vmem_limit_bytes=60 * 1024 * 1024),
            name="sinkhorn",
        )(kernel, cost_mat, src_mass.T, tgt_mass.T)
        u_t, v_t, cost = pl.pallas_call(
            lambda *refs: output_kernel(norm, *refs),
            out_shape=(jax.ShapeDtypeStruct((nprob, rows), F32), jax.ShapeDtypeStruct((nprob, half), F32),
                       jax.ShapeDtypeStruct((1, nprob), F32)),
            in_specs=[vmem_spec] * 3,
            out_specs=(any_spec, any_spec, vmem_spec),
            scratch_shapes=[dma((2,))],
            name="outputs",
        )(*(pltpu.with_memory_space_constraint(r, pltpu.VMEM) for r in (u_vm, v_vm, c_vm)))
        return u_t.T, v_t.T, cost.reshape(nprob)

    return jax.shard_map(local_fn, mesh=mesh, in_specs=(P("row", "col"), P("row", "col"), P("row", "prob"), P("col", "prob")), out_specs=(P("row", "prob"), P("col", "prob"), P("prob")), check_vma=False)
```

time: 60.5 us -> 59.7 us (0.987)
  Pallas kernels: 59.8 us -> 59 us
    pallas_call x1, Pallas kernels: 58.5 us -> 57.7 us  [local_fn(): pl.pallas_call(lambda *refs: sinkhorn_kernel(n_chunk, *refs), out_shape=(...]
where the time goes in v6:
time: 59.7 us; the launch traced here: 59.6 us
  Pallas kernels  59 us (99%)
  between operations  0.64 us (1%)
    pallas_call x1, Pallas kernels, local_fn(): pl.pallas_call(lambda *refs: sinkhorn_kernel(n_chunk, *refs), out_shape=(...  57.7 us
    pallas_call x1, Pallas kernels, local_fn(): pl.pallas_call(lambda *refs: output_kernel(norm, *refs), out_shape=(jax.S...  1.27 us

profile of v6, /device:TPU:0, one launch (start us, length us, event | category | flops | bytes accessed | tf_op | source)
XLA Modules:
  0.0 59.6 jit_solution(17772141133230930642)
XLA Ops:
  0.6 57.7 %sinkhorn.1 = (f32[32,2048]{1,0:T(8,128)S(1)}, f32[32,1024]{1,0:T(8,128)S(1)}, f32[8,1,128]{2,1,0:T(1,128)S(1)}) custom-call(bf16[2048,1024]{1,0:T(8,128)(2,1)} %refs_0_.1, bf16[2048,1024]{1,0:T(8,128)(2,1)} %refs_1_.1, f32[32,2048]{1,0:T(8,128)} %bitcast.5, f32[32,1024]{1,0:T(8,128)} %bitcast.6), custom_call_target="tpu_custom_call" | custom-call | tf_op jit(solution)/shard_map/sinkhorn/pallas_call | solution.py:296
  58.4 1.3 %outputs.1 = (f32[32,2048]{1,0:T(8,128)}, f32[32,1024]{1,0:T(8,128)}, f32[1,32]{1,0:T(1,128)}) custom-call(f32[32,2048]{1,0:T(8,128)S(1)} %get-tuple-element.9.refs_0_, f32[32,1024]{1,0:T(8,128)S(1)} %get-tuple-element.10.refs_1_, f32[8,1,128]{2,1,0:T(1,128)S(1)} %get-tuple-element.11.refs_2_), custom_call_target="tpu_custom_call" | custom-call | tf_op jit(solution)/shard_map/outputs/pallas_call | solution.py:323

commit v7 on v6

--- a/solution.py
+++ b/solution.py
@@ -97,22 +97,20 @@
 
     k_push = [remote(k_buf.at[core, krows(i)], k_buf.at[core, krows(i)], send_sem.at[KP], kp_recv.at[i], partner) for i in range(n_chunk)]
     b_push = remote(b_hbm.at[other], b_buf.at[core], send_sem.at[BP], one_recv.at[0], partner)
-    pl.semaphore_wait(barrier, 7)
-    b_push.start()
     ones = jnp.ones((nq, half), BF16)
     for i in range(n_chunk):
         k_load[i].wait()
-        if i == 0:
-            k_push[0].start()
         if i % 2:
             part = lax.dot_general(ones, k_buf[core, pl.ds((i - 1) * rw, 2 * rw)], (((1,), (1,)), ((), ())), preferred_element_type=F32)
             for n in range(2 * rw // 128):
                 r = (i - 1) * (rw // 128) + n
                 s0_buf[col, r:r + 1, :] = part[0:1, n * 128:(n + 1) * 128]
+    pl.semaphore_wait(barrier, 7)
     for n in range(1, 4):
         remote(s0_buf.at[col], s0_buf.at[col], send_sem.at[S0], one_recv.at[1], dev(row, (col + n) % 4)).start()
-    for i in range(1, n_chunk):
-        k_push[i].start()
+    b_push.start()
+    for d in k_push:
+        d.start()
     for d in c_load:
         d.start()
     for i in range(n_chunk):
@@ -157,7 +155,7 @@
 
     @pl.when(grp == 1)
     def _():
-        for i in range(n_chunk):
+        for i in range(per_half):
             build_kct(i)
 
     all_here(t0_buf.at[0], one_recv.at[2])
@@ -179,10 +177,8 @@
     all_sent(k_buf.at[0], KP)
     all_sent(b_buf.at[0], BP)
 
-    @pl.when(grp == 0)
-    def _():
-        for i in range(n_chunk - 1):
-            build_kct(i)
+    for i in range(per_half):
+        build_kct(i + grp * per_half)
 
     def u_and_t(par):
         for c in range(n_chunk):
@@ -224,7 +220,8 @@
 
         @pl.when((grp == 0) & (t == 1))
         def _():
-            build_kct(n_chunk - 1)
+            for i in range(per_half, n_chunk):
+                build_kct(i)
 
         v_and_s(t % 2, (t + 1) % 2)
         return carry

time: 59.7 us -> 66.2 us (1.11)
  Pallas kernels: 59 us -> 65.4 us
    pallas_call x1, Pallas kernels: 57.7 us -> 64.1 us  [local_fn(): pl.pallas_call(lambda *refs: sinkhorn_kernel(n_chunk, *refs), out_shape=(...]
where the time goes in v7:
time: 66.2 us; the launch traced here: 66.1 us
  Pallas kernels  65.4 us (99%)
    pallas_call x1, Pallas kernels, local_fn(): pl.pallas_call(lambda *refs: sinkhorn_kernel(n_chunk, *refs), out_shape=(...  64.1 us

profile of v7, /device:TPU:0, one launch (start us, length us, event | category | flops | bytes accessed | tf_op | source)
XLA Modules:
  0.0 66.1 jit_solution(2935773699557890337)
XLA Ops:
  0.6 64.1 %sinkhorn.1 = (f32[32,2048]{1,0:T(8,128)S(1)}, f32[32,1024]{1,0:T(8,128)S(1)}, f32[8,1,128]{2,1,0:T(1,128)S(1)}) custom-call(bf16[2048,1024]{1,0:T(8,128)(2,1)} %refs_0_.1, bf16[2048,1024]{1,0:T(8,128)(2,1)} %refs_1_.1, f32[32,2048]{1,0:T(8,128)} %bitcast.5, f32[32,1024]{1,0:T(8,128)} %bitcast.6), custom_call_target="tpu_custom_call" | custom-call | tf_op jit(solution)/shard_map/sinkhorn/pallas_call | solution.py:293
  64.8 1.3 %outputs.1 = (f32[32,2048]{1,0:T(8,128)}, f32[32,1024]{1,0:T(8,128)}, f32[1,32]{1,0:T(1,128)}) custom-call(f32[32,2048]{1,0:T(8,128)S(1)} %get-tuple-element.9.refs_0_, f32[32,1024]{1,0:T(8,128)S(1)} %get-tuple-element.10.refs_1_, f32[8,1,128]{2,1,0:T(1,128)S(1)} %get-tuple-element.11.refs_2_), custom_call_target="tpu_custom_call" | custom-call | tf_op jit(solution)/shard_map/outputs/pallas_call | solution.py:320

commit v8 on v6

--- a/solution.py
+++ b/solution.py
@@ -157,7 +157,7 @@
 
     @pl.when(grp == 1)
     def _():
-        for i in range(n_chunk):
+        for i in range(n_chunk - 1):
             build_kct(i)
 
     all_here(t0_buf.at[0], one_recv.at[2])
@@ -181,8 +181,12 @@
 
     @pl.when(grp == 0)
     def _():
-        for i in range(n_chunk - 1):
+        for i in range(per_half):
             build_kct(i)
+
+    @pl.when(grp == 1)
+    def _():
+        build_kct(n_chunk - 1)
 
     def u_and_t(par):
         for c in range(n_chunk):
@@ -224,7 +228,8 @@
 
         @pl.when((grp == 0) & (t == 1))
         def _():
-            build_kct(n_chunk - 1)
+            for i in range(per_half, n_chunk):
+                build_kct(i)
 
         v_and_s(t % 2, (t + 1) % 2)
         return carry

time: 59.7 us -> 59.8 us (level)
  no operation moved by 1% of the time
where the time goes in v8:
time: 59.8 us; the launch traced here: 59.7 us
  Pallas kernels  59 us (99%)
  between operations  0.64 us (1%)
    pallas_call x1, Pallas kernels, local_fn(): pl.pallas_call(lambda *refs: sinkhorn_kernel(n_chunk, *refs), out_shape=(...  57.8 us
    pallas_call x1, Pallas kernels, local_fn(): pl.pallas_call(lambda *refs: output_kernel(norm, *refs), out_shape=(jax.S...  1.27 us

profile of v8, /device:TPU:0, one launch (start us, length us, event | category | flops | bytes accessed | tf_op | source)
XLA Modules:
  0.0 59.7 jit_solution(8423719658561277358)
XLA Ops:
  0.6 57.8 %sinkhorn.1 = (f32[32,2048]{1,0:T(8,128)S(1)}, f32[32,1024]{1,0:T(8,128)S(1)}, f32[8,1,128]{2,1,0:T(1,128)S(1)}) custom-call(bf16[2048,1024]{1,0:T(8,128)(2,1)} %refs_0_.1, bf16[2048,1024]{1,0:T(8,128)(2,1)} %refs_1_.1, f32[32,2048]{1,0:T(8,128)} %bitcast.5, f32[32,1024]{1,0:T(8,128)} %bitcast.6), custom_call_target="tpu_custom_call" | custom-call | tf_op jit(solution)/shard_map/sinkhorn/pallas_call | solution.py:301
  58.4 1.3 %outputs.1 = (f32[32,2048]{1,0:T(8,128)}, f32[32,1024]{1,0:T(8,128)}, f32[1,32]{1,0:T(1,128)}) custom-call(f32[32,2048]{1,0:T(8,128)S(1)} %get-tuple-element.9.refs_0_, f32[32,1024]{1,0:T(8,128)S(1)} %get-tuple-element.10.refs_1_, f32[8,1,128]{2,1,0:T(1,128)S(1)} %get-tuple-element.11.refs_2_), custom_call_target="tpu_custom_call" | custom-call | tf_op jit(solution)/shard_map/outputs/pallas_call | solution.py:328

commit v9 on v8

--- a/solution.py
+++ b/solution.py
@@ -160,6 +160,10 @@
         for i in range(n_chunk - 1):
             build_kct(i)
 
+    @pl.when((grp == 1) & (core == 0))
+    def _():
+        build_kct(n_chunk - 1)
+
     all_here(t0_buf.at[0], one_recv.at[2])
     order = list(range(per_half, n_chunk)) + list(range(per_half))
     for c in order:
@@ -184,7 +188,7 @@
         for i in range(per_half):
             build_kct(i)
 
-    @pl.when(grp == 1)
+    @pl.when((grp == 1) & (core == 1))
     def _():
         build_kct(n_chunk - 1)
 

time: 59.8 us -> 59.2 us (0.990)
  no operation moved by 1% of the time
where the time goes in v9:
time: 59.2 us; the launch traced here: 59.1 us
  Pallas kernels  58.5 us (99%)
  between operations  0.64 us (1%)
    pallas_call x1, Pallas kernels, local_fn(): pl.pallas_call(lambda *refs: sinkhorn_kernel(n_chunk, *refs), out_shape=(...  57.2 us
    pallas_call x1, Pallas kernels, local_fn(): pl.pallas_call(lambda *refs: output_kernel(norm, *refs), out_shape=(jax.S...  1.27 us

profile of v9, /device:TPU:0, one launch (start us, length us, event | category | flops | bytes accessed | tf_op | source)
XLA Modules:
  0.0 59.1 jit_solution(12842719730296017876)
XLA Ops:
  0.6 57.2 %sinkhorn.1 = (f32[32,2048]{1,0:T(8,128)S(1)}, f32[32,1024]{1,0:T(8,128)S(1)}, f32[8,1,128]{2,1,0:T(1,128)S(1)}) custom-call(bf16[2048,1024]{1,0:T(8,128)(2,1)} %refs_0_.1, bf16[2048,1024]{1,0:T(8,128)(2,1)} %refs_1_.1, f32[32,2048]{1,0:T(8,128)} %bitcast.5, f32[32,1024]{1,0:T(8,128)} %bitcast.6), custom_call_target="tpu_custom_call" | custom-call | tf_op jit(solution)/shard_map/sinkhorn/pallas_call | solution.py:305
  57.9 1.3 %outputs.1 = (f32[32,2048]{1,0:T(8,128)}, f32[32,1024]{1,0:T(8,128)}, f32[1,32]{1,0:T(1,128)}) custom-call(f32[32,2048]{1,0:T(8,128)S(1)} %get-tuple-element.9.refs_0_, f32[32,1024]{1,0:T(8,128)S(1)} %get-tuple-element.10.refs_1_, f32[8,1,128]{2,1,0:T(1,128)S(1)} %get-tuple-element.11.refs_2_), custom_call_target="tpu_custom_call" | custom-call | tf_op jit(solution)/shard_map/outputs/pallas_call | solution.py:332

commit v10 on v9

--- a/solution.py
+++ b/solution.py
@@ -57,10 +57,8 @@
     c_load = [pltpu.make_async_copy(c_hbm.at[krows(i)], c_buf.at[krows(i)], load_sem.at[i]) for i in range(n_chunk)]
     a_load = pltpu.make_async_copy(a_hbm, a_buf, load_sem.at[n_chunk])
     b_load = pltpu.make_async_copy(b_hbm.at[mine], b_buf.at[core], load_sem.at[n_chunk + 1])
-    for d in k_load:
-        d.start()
-    a_load.start()
-    b_load.start()
+    for d in k_load[:per_half]:
+        d.start()
 
     barrier = pltpu.get_barrier_semaphore()
     for dr in range(2):
@@ -97,22 +95,32 @@
 
     k_push = [remote(k_buf.at[core, krows(i)], k_buf.at[core, krows(i)], send_sem.at[KP], kp_recv.at[i], partner) for i in range(n_chunk)]
     b_push = remote(b_hbm.at[other], b_buf.at[core], send_sem.at[BP], one_recv.at[0], partner)
+    ones = jnp.ones((nq, half), BF16)
+
+    def first_s(i):
+        part = lax.dot_general(ones, k_buf[core, pl.ds(i * rw, per_half * rw)], (((1,), (1,)), ((), ())), preferred_element_type=F32)
+        for n in range(per_half * rw // 128):
+            r = i * (rw // 128) + n
+            s0_buf[col, r:r + 1, :] = part[0:1, n * 128:(n + 1) * 128]
+
+    for d in k_load[:per_half]:
+        d.wait()
+    for d in k_load[per_half:]:
+        d.start()
+    a_load.start()
+    b_load.start()
+    first_s(0)
     pl.semaphore_wait(barrier, 7)
     b_push.start()
-    ones = jnp.ones((nq, half), BF16)
-    for i in range(n_chunk):
-        k_load[i].wait()
-        if i == 0:
-            k_push[0].start()
-        if i % 2:
-            part = lax.dot_general(ones, k_buf[core, pl.ds((i - 1) * rw, 2 * rw)], (((1,), (1,)), ((), ())), preferred_element_type=F32)
-            for n in range(2 * rw // 128):
-                r = (i - 1) * (rw // 128) + n
-                s0_buf[col, r:r + 1, :] = part[0:1, n * 128:(n + 1) * 128]
+    for d in k_push[:per_half]:
+        d.start()
+    for d in k_load[per_half:]:
+        d.wait()
+    first_s(per_half)
     for n in range(1, 4):
         remote(s0_buf.at[col], s0_buf.at[col], send_sem.at[S0], one_recv.at[1], dev(row, (col + n) % 4)).start()
-    for i in range(1, n_chunk):
-        k_push[i].start()
+    for d in k_push[per_half:]:
+        d.start()
     for d in c_load:
         d.start()
     for i in range(n_chunk):

time: 59.2 us -> 65.1 us (1.100)
  Pallas kernels: 58.5 us -> 64.3 us
    pallas_call x1, Pallas kernels: 57.2 us -> 63.1 us  [local_fn(): pl.pallas_call(lambda *refs: sinkhorn_kernel(n_chunk, *refs), out_shape=(...]
where the time goes in v10:
time: 65.1 us; the launch traced here: 65 us
  Pallas kernels  64.3 us (99%)
    pallas_call x1, Pallas kernels, local_fn(): pl.pallas_call(lambda *refs: sinkhorn_kernel(n_chunk, *refs), out_shape=(...  63.1 us

profile of v10, /device:TPU:0, one launch (start us, length us, event | category | flops | bytes accessed | tf_op | source)
XLA Modules:
  0.0 65.0 jit_solution(4891312957567515894)
XLA Ops:
  0.6 63.1 %sinkhorn.1 = (f32[32,2048]{1,0:T(8,128)S(1)}, f32[32,1024]{1,0:T(8,128)S(1)}, f32[8,1,128]{2,1,0:T(1,128)S(1)}) custom-call(bf16[2048,1024]{1,0:T(8,128)(2,1)} %refs_0_.1, bf16[2048,1024]{1,0:T(8,128)(2,1)} %refs_1_.1, f32[32,2048]{1,0:T(8,128)} %bitcast.5, f32[32,1024]{1,0:T(8,128)} %bitcast.6), custom_call_target="tpu_custom_call" | custom-call | tf_op jit(solution)/shard_map/sinkhorn/pallas_call | solution.py:313
  63.7 1.3 %outputs.1 = (f32[32,2048]{1,0:T(8,128)}, f32[32,1024]{1,0:T(8,128)}, f32[1,32]{1,0:T(1,128)}) custom-call(f32[32,2048]{1,0:T(8,128)S(1)} %get-tuple-element.9.refs_0_, f32[32,1024]{1,0:T(8,128)S(1)} %get-tuple-element.10.refs_1_, f32[8,1,128]{2,1,0:T(1,128)S(1)} %get-tuple-element.11.refs_2_), custom_call_target="tpu_custom_call" | custom-call | tf_op jit(solution)/shard_map/outputs/pallas_call | solution.py:340

commit v11 on v6

--- a/solution.py
+++ b/solution.py
@@ -6,6 +6,7 @@
 from jax.sharding import PartitionSpec as P
 
 SWEEPS = 6
+AHEAD = (7, 5)
 F32 = jnp.float32
 BF16 = jnp.bfloat16
 MESH = pl.DeviceIdType.MESH
@@ -79,21 +80,22 @@
             return carry
         lax.fori_loop(0, half // blk, body, 0)
 
-    def kct_copy(i):
-        part = kct_buf.at[pl.ds(pl.multiple_of(core * half, half), half), pl.ds(pl.multiple_of(i * rw, rw), rw)]
-        return remote(part, part, send_sem.at[KC], one_recv.at[5], partner)
-
-    def build_kct(i):
-        pltpu.make_async_copy(c_hbm.at[pl.ds(i * rw, rw)], c_buf.at[pl.ds(i * rw, rw)], load_sem.at[i]).wait()
-        def body(n, carry):
-            jo = pl.multiple_of(n * blk, blk)
-            for ii in range(rw // blk):
-                rs = pl.ds(pl.multiple_of(i * rw + ii * blk, blk), blk)
-                kct_buf[pl.ds(pl.multiple_of(core * half + jo, blk), blk), rs] = (
-                    k_buf[core, rs, pl.ds(jo, blk)] * c_buf[rs, pl.ds(jo, blk)]).T
+    kct_pieces = 2 * n_chunk
+    kw = rows // kct_pieces
+
+    def build_kct(lo, hi):
+        def piece(i, carry):
+            rs = pl.ds(pl.multiple_of(i * kw, kw), kw)
+            for n in range(half // blk):
+                kct_buf[pl.ds(pl.multiple_of(core * half + n * blk, blk), blk), rs] = (
+                    k_buf[core, rs, n * blk:(n + 1) * blk] * c_buf[rs, n * blk:(n + 1) * blk]).T
+            part = kct_buf.at[pl.ds(pl.multiple_of(core * half, half), half), rs]
+            remote(part, part, send_sem.at[KC], one_recv.at[5], partner).start()
             return carry
-        lax.fori_loop(0, half // blk, body, 0)
-        kct_copy(i).start()
+        lax.fori_loop(lo, hi, piece, 0)
+
+    ahead = grp * (AHEAD[0] + core * (AHEAD[1] - AHEAD[0]))
+    middle = grp * kct_pieces + (1 - grp) * (kct_pieces // 2)
 
     k_push = [remote(k_buf.at[core, krows(i)], k_buf.at[core, krows(i)], send_sem.at[KP], kp_recv.at[i], partner) for i in range(n_chunk)]
     b_push = remote(b_hbm.at[other], b_buf.at[core], send_sem.at[BP], one_recv.at[0], partner)
@@ -141,8 +143,6 @@
             t0_buf[g, n] = part[g * nq:(g + 1) * nq]
         t0_send(0, n)
     for n in range(per_half):
-        t0_send(1, n)
-    for n in range(per_half):
         o = core * per_half + n
         remote(t0_buf.at[1 - grp, n], t_out.at[o], send_sem.at[TP], one_recv.at[2], partner).start()
         t_out[o] = t0_buf[grp, n]
@@ -154,11 +154,13 @@
     for i in range(n_chunk):
         all_here(k_buf.at[1 - core, krows(i)], kp_recv.at[i])
         transpose_rows(1 - core, i)
-
-    @pl.when(grp == 1)
-    def _():
-        for i in range(n_chunk):
-            build_kct(i)
+        if i == 0:
+            for n in range(per_half):
+                t0_send(1, n)
+
+    for d in c_load:
+        d.wait()
+    build_kct(0, ahead)
 
     all_here(t0_buf.at[0], one_recv.at[2])
     order = list(range(per_half, n_chunk)) + list(range(per_half))
@@ -179,10 +181,7 @@
     all_sent(k_buf.at[0], KP)
     all_sent(b_buf.at[0], BP)
 
-    @pl.when(grp == 0)
-    def _():
-        for i in range(n_chunk - 1):
-            build_kct(i)
+    build_kct(ahead, middle)
 
     def u_and_t(par):
         for c in range(n_chunk):
@@ -197,12 +196,12 @@
                     prod = jnp.dot(ub, k_buf[h, w, :], preferred_element_type=F32)
                     acc[:, hc] = prod if c == 0 else acc[:, hc] + prod
             else:
-                all_sent(s_out, SS)
                 for o in range(n_chunk):
                     oc = slice(o * cw, (o + 1) * cw)
                     hc = slice((o % per_half) * cw, (o % per_half + 1) * cw)
                     t_out[o] = acc[:, oc] + jnp.dot(ub, k_buf[o // per_half, w, hc], preferred_element_type=F32)
                     t_copy(par, o).start()
+                all_sent(s_out, SS)
 
     def v_and_s(par_in, par):
         for c in range(n_chunk):
@@ -213,18 +212,18 @@
                 prod = jnp.dot(vb, kt_buf[w, :], preferred_element_type=F32)
                 acc[...] = prod if c == 0 else acc[...] + prod
             else:
-                all_sent(t_out, TT)
                 for o in range(n_chunk):
                     oc = slice(o * rw, (o + 1) * rw)
                     s_out[o] = acc[:, oc] + jnp.dot(vb, kt_buf[w, oc], preferred_element_type=F32)
                     s_copy(par, o).start()
+                all_sent(t_out, TT)
 
     def sweep(t, carry):
         u_and_t(t % 2)
 
-        @pl.when((grp == 0) & (t == 1))
+        @pl.when(t == 1)
         def _():
-            build_kct(n_chunk - 1)
+            build_kct(middle, kct_pieces)
 
         v_and_s(t % 2, (t + 1) % 2)
         return carry

time: 59.7 us -> 64 us (1.072)
  Pallas kernels: 59 us -> 63.3 us
    pallas_call x1, Pallas kernels: 57.7 us -> 62 us  [local_fn(): pl.pallas_call(lambda *refs: sinkhorn_kernel(n_chunk, *refs), out_shape=(...]
where the time goes in v11:
time: 64 us; the launch traced here: 63.9 us
  Pallas kernels  63.3 us (99%)
  between operations  0.64 us (1%)
    pallas_call x1, Pallas kernels, local_fn(): pl.pallas_call(lambda *refs: sinkhorn_kernel(n_chunk, *refs), out_shape=(...  62 us

profile of v11, /device:TPU:0, one launch (start us, length us, event | category | flops | bytes accessed | tf_op | source)
XLA Modules:
  0.0 63.9 jit_solution(4998136427553191887)
XLA Ops:
  0.6 62.0 %sinkhorn.1 = (f32[32,2048]{1,0:T(8,128)S(1)}, f32[32,1024]{1,0:T(8,128)S(1)}, f32[8,1,128]{2,1,0:T(1,128)S(1)}) custom-call(bf16[2048,1024]{1,0:T(8,128)(2,1)} %refs_0_.1, bf16[2048,1024]{1,0:T(8,128)(2,1)} %refs_1_.1, f32[32,2048]{1,0:T(8,128)} %bitcast.5, f32[32,1024]{1,0:T(8,128)} %bitcast.6), custom_call_target="tpu_custom_call" | custom-call | tf_op jit(solution)/shard_map/sinkhorn/pallas_call | solution.py:295
  62.7 1.3 %outputs.1 = (f32[32,2048]{1,0:T(8,128)}, f32[32,1024]{1,0:T(8,128)}, f32[1,32]{1,0:T(1,128)}) custom-call(f32[32,2048]{1,0:T(8,128)S(1)} %get-tuple-element.9.refs_0_, f32[32,1024]{1,0:T(8,128)S(1)} %get-tuple-element.10.refs_1_, f32[8,1,128]{2,1,0:T(1,128)S(1)} %get-tuple-element.11.refs_2_), custom_call_target="tpu_custom_call" | custom-call | tf_op jit(solution)/shard_map/outputs/pallas_call | solution.py:322

commit v12 on v11

--- a/solution.py
+++ b/solution.py
@@ -6,7 +6,8 @@
 from jax.sharding import PartitionSpec as P
 
 SWEEPS = 6
-AHEAD = (7, 5)
+AHEAD = (8, 6)
+WAIT_NS = 700
 F32 = jnp.float32
 BF16 = jnp.bfloat16
 MESH = pl.DeviceIdType.MESH
@@ -161,6 +162,10 @@
     for d in c_load:
         d.wait()
     build_kct(0, ahead)
+
+    @pl.when(grp == 1)
+    def _():
+        pl.delay(WAIT_NS)
 
     all_here(t0_buf.at[0], one_recv.at[2])
     order = list(range(per_half, n_chunk)) + list(range(per_half))

time: 64 us -> 58.9 us (0.920)
  Pallas kernels: 63.3 us -> 58.1 us
    pallas_call x1, Pallas kernels: 62 us -> 56.8 us  [local_fn(): pl.pallas_call(lambda *refs: sinkhorn_kernel(n_chunk, *refs), out_shape=(...]
where the time goes in v12:
time: 58.9 us; the launch traced here: 58.8 us
  Pallas kernels  58.1 us (99%)
  between operations  0.64 us (1%)
    pallas_call x1, Pallas kernels, local_fn(): pl.pallas_call(lambda *refs: sinkhorn_kernel(n_chunk, *refs), out_shape=(...  56.8 us
    pallas_call x1, Pallas kernels, local_fn(): pl.pallas_call(lambda *refs: output_kernel(norm, *refs), out_shape=(jax.S...  1.27 us

profile of v12, /device:TPU:0, one launch (start us, length us, event | category | flops | bytes accessed | tf_op | source)
XLA Modules:
  0.0 58.8 jit_solution(10117026489827382920)
XLA Ops:
  0.6 56.8 %sinkhorn.1 = (f32[32,2048]{1,0:T(8,128)S(1)}, f32[32,1024]{1,0:T(8,128)S(1)}, f32[8,1,128]{2,1,0:T(1,128)S(1)}) custom-call(bf16[2048,1024]{1,0:T(8,128)(2,1)} %refs_0_.1, bf16[2048,1024]{1,0:T(8,128)(2,1)} %refs_1_.1, f32[32,2048]{1,0:T(8,128)} %bitcast.5, f32[32,1024]{1,0:T(8,128)} %bitcast.6), custom_call_target="tpu_custom_call" | custom-call | tf_op jit(solution)/shard_map/sinkhorn/pallas_call | solution.py:300
  57.5 1.3 %outputs.1 = (f32[32,2048]{1,0:T(8,128)}, f32[32,1024]{1,0:T(8,128)}, f32[1,32]{1,0:T(1,128)}) custom-call(f32[32,2048]{1,0:T(8,128)S(1)} %get-tuple-element.9.refs_0_, f32[32,1024]{1,0:T(8,128)S(1)} %get-tuple-element.10.refs_1_, f32[8,1,128]{2,1,0:T(1,128)S(1)} %get-tuple-element.11.refs_2_), custom_call_target="tpu_custom_call" | custom-call | tf_op jit(solution)/shard_map/outputs/pallas_call | solution.py:327

commit v13 on v12

--- a/solution.py
+++ b/solution.py
@@ -7,7 +7,7 @@
 
 SWEEPS = 6
 AHEAD = (8, 6)
-WAIT_NS = 700
+WAIT_NS = 1000
 F32 = jnp.float32
 BF16 = jnp.bfloat16
 MESH = pl.DeviceIdType.MESH

time: 58.9 us -> 59.3 us (level)
  no operation moved by 1% of the time
where the time goes in v13:
time: 59.3 us; the launch traced here: 59.2 us
  Pallas kernels  58.6 us (99%)
  between operations  0.64 us (1%)
    pallas_call x1, Pallas kernels, local_fn(): pl.pallas_call(lambda *refs: sinkhorn_kernel(n_chunk, *refs), out_shape=(...  57.3 us
    pallas_call x1, Pallas kernels, local_fn(): pl.pallas_call(lambda *refs: output_kernel(norm, *refs), out_shape=(jax.S...  1.27 us

profile of v13, /device:TPU:0, one launch (start us, length us, event | category | flops | bytes accessed | tf_op | source)
XLA Modules:
  0.0 59.2 jit_solution(10483163089892840603)
XLA Ops:
  0.6 57.3 %sinkhorn.1 = (f32[32,2048]{1,0:T(8,128)S(1)}, f32[32,1024]{1,0:T(8,128)S(1)}, f32[8,1,128]{2,1,0:T(1,128)S(1)}) custom-call(bf16[2048,1024]{1,0:T(8,128)(2,1)} %refs_0_.1, bf16[2048,1024]{1,0:T(8,128)(2,1)} %refs_1_.1, f32[32,2048]{1,0:T(8,128)} %bitcast.5, f32[32,1024]{1,0:T(8,128)} %bitcast.6), custom_call_target="tpu_custom_call" | custom-call | tf_op jit(solution)/shard_map/sinkhorn/pallas_call | solution.py:300
  58.0 1.3 %outputs.1 = (f32[32,2048]{1,0:T(8,128)}, f32[32,1024]{1,0:T(8,128)}, f32[1,32]{1,0:T(1,128)}) custom-call(f32[32,2048]{1,0:T(8,128)S(1)} %get-tuple-element.9.refs_0_, f32[32,1024]{1,0:T(8,128)S(1)} %get-tuple-element.10.refs_1_, f32[8,1,128]{2,1,0:T(1,128)S(1)} %get-tuple-element.11.refs_2_), custom_call_target="tpu_custom_call" | custom-call | tf_op jit(solution)/shard_map/outputs/pallas_call | solution.py:327

commit v14 on v13

--- a/solution.py
+++ b/solution.py
@@ -7,7 +7,7 @@
 
 SWEEPS = 6
 AHEAD = (8, 6)
-WAIT_NS = 1000
+WAIT_NS = 850
 F32 = jnp.float32
 BF16 = jnp.bfloat16
 MESH = pl.DeviceIdType.MESH

time: 59.3 us -> 59.2 us (level)
  no operation moved by 1% of the time
where the time goes in v14:
time: 59.2 us; the launch traced here: 59.1 us
  Pallas kernels  58.4 us (99%)
  between operations  0.64 us (1%)
    pallas_call x1, Pallas kernels, local_fn(): pl.pallas_call(lambda *refs: sinkhorn_kernel(n_chunk, *refs), out_shape=(...  57.2 us
    pallas_call x1, Pallas kernels, local_fn(): pl.pallas_call(lambda *refs: output_kernel(norm, *refs), out_shape=(jax.S...  1.27 us

profile of v14, /device:TPU:0, one launch (start us, length us, event | category | flops | bytes accessed | tf_op | source)
XLA Modules:
  0.0 59.1 jit_solution(14821374352280330789)
XLA Ops:
  0.6 57.2 %sinkhorn.1 = (f32[32,2048]{1,0:T(8,128)S(1)}, f32[32,1024]{1,0:T(8,128)S(1)}, f32[8,1,128]{2,1,0:T(1,128)S(1)}) custom-call(bf16[2048,1024]{1,0:T(8,128)(2,1)} %refs_0_.1, bf16[2048,1024]{1,0:T(8,128)(2,1)} %refs_1_.1, f32[32,2048]{1,0:T(8,128)} %bitcast.5, f32[32,1024]{1,0:T(8,128)} %bitcast.6), custom_call_target="tpu_custom_call" | custom-call | tf_op jit(solution)/shard_map/sinkhorn/pallas_call | solution.py:300
  57.8 1.3 %outputs.1 = (f32[32,2048]{1,0:T(8,128)}, f32[32,1024]{1,0:T(8,128)}, f32[1,32]{1,0:T(1,128)}) custom-call(f32[32,2048]{1,0:T(8,128)S(1)} %get-tuple-element.9.refs_0_, f32[32,1024]{1,0:T(8,128)S(1)} %get-tuple-element.10.refs_1_, f32[8,1,128]{2,1,0:T(1,128)S(1)} %get-tuple-element.11.refs_2_), custom_call_target="tpu_custom_call" | custom-call | tf_op jit(solution)/shard_map/outputs/pallas_call | solution.py:327

commit v15 on v14

--- a/solution.py
+++ b/solution.py
@@ -7,7 +7,7 @@
 
 SWEEPS = 6
 AHEAD = (8, 6)
-WAIT_NS = 850
+WAIT_NS = 550
 F32 = jnp.float32
 BF16 = jnp.bfloat16
 MESH = pl.DeviceIdType.MESH

time: 59.2 us -> 58.6 us (0.990)
  no operation moved by 1% of the time
where the time goes in v15:
time: 58.6 us; the launch traced here: 58.5 us
  Pallas kernels  57.9 us (99%)
  between operations  0.64 us (1%)
    pallas_call x1, Pallas kernels, local_fn(): pl.pallas_call(lambda *refs: sinkhorn_kernel(n_chunk, *refs), out_shape=(...  56.6 us
    pallas_call x1, Pallas kernels, local_fn(): pl.pallas_call(lambda *refs: output_kernel(norm, *refs), out_shape=(jax.S...  1.27 us

profile of v15, /device:TPU:0, one launch (start us, length us, event | category | flops | bytes accessed | tf_op | source)
XLA Modules:
  0.0 58.5 jit_solution(6580491566353018253)
XLA Ops:
  0.6 56.6 %sinkhorn.1 = (f32[32,2048]{1,0:T(8,128)S(1)}, f32[32,1024]{1,0:T(8,128)S(1)}, f32[8,1,128]{2,1,0:T(1,128)S(1)}) custom-call(bf16[2048,1024]{1,0:T(8,128)(2,1)} %refs_0_.1, bf16[2048,1024]{1,0:T(8,128)(2,1)} %refs_1_.1, f32[32,2048]{1,0:T(8,128)} %bitcast.5, f32[32,1024]{1,0:T(8,128)} %bitcast.6), custom_call_target="tpu_custom_call" | custom-call | tf_op jit(solution)/shard_map/sinkhorn/pallas_call | solution.py:300
  57.2 1.3 %outputs.1 = (f32[32,2048]{1,0:T(8,128)}, f32[32,1024]{1,0:T(8,128)}, f32[1,32]{1,0:T(1,128)}) custom-call(f32[32,2048]{1,0:T(8,128)S(1)} %get-tuple-element.9.refs_0_, f32[32,1024]{1,0:T(8,128)S(1)} %get-tuple-element.10.refs_1_, f32[8,1,128]{2,1,0:T(1,128)S(1)} %get-tuple-element.11.refs_2_), custom_call_target="tpu_custom_call" | custom-call | tf_op jit(solution)/shard_map/outputs/pallas_call | solution.py:327

commit v16 on v11

--- a/solution.py
+++ b/solution.py
@@ -6,7 +6,8 @@
 from jax.sharding import PartitionSpec as P
 
 SWEEPS = 6
-AHEAD = (7, 5)
+AHEAD = (8, 7)
+WAIT_NS = ((0, 350), (650, 600))
 F32 = jnp.float32
 BF16 = jnp.bfloat16
 MESH = pl.DeviceIdType.MESH
@@ -161,6 +162,13 @@
     for d in c_load:
         d.wait()
     build_kct(0, ahead)
+
+    for g in range(2):
+        for c in range(2):
+            if WAIT_NS[g][c]:
+                @pl.when((grp == g) & (core == c))
+                def _(g=g, c=c):
+                    pl.delay(WAIT_NS[g][c])
 
     all_here(t0_buf.at[0], one_recv.at[2])
     order = list(range(per_half, n_chunk)) + list(range(per_half))

time: 64 us -> 59.1 us (0.923)
  Pallas kernels: 63.3 us -> 58.4 us
    pallas_call x1, Pallas kernels: 62 us -> 57.1 us  [local_fn(): pl.pallas_call(lambda *refs: sinkhorn_kernel(n_chunk, *refs), out_shape=(...]
where the time goes in v16:
time: 59.1 us; the launch traced here: 59 us
  Pallas kernels  58.4 us (99%)
  between operations  0.64 us (1%)
    pallas_call x1, Pallas kernels, local_fn(): pl.pallas_call(lambda *refs: sinkhorn_kernel(n_chunk, *refs), out_shape=(...  57.1 us
    pallas_call x1, Pallas kernels, local_fn(): pl.pallas_call(lambda *refs: output_kernel(norm, *refs), out_shape=(jax.S...  1.27 us

profile of v16, /device:TPU:0, one launch (start us, length us, event | category | flops | bytes accessed | tf_op | source)
XLA Modules:
  0.0 59.0 jit_solution(15990318672635029444)
XLA Ops:
  0.6 57.1 %sinkhorn.1 = (f32[32,2048]{1,0:T(8,128)S(1)}, f32[32,1024]{1,0:T(8,128)S(1)}, f32[8,1,128]{2,1,0:T(1,128)S(1)}) custom-call(bf16[2048,1024]{1,0:T(8,128)(2,1)} %refs_0_.1, bf16[2048,1024]{1,0:T(8,128)(2,1)} %refs_1_.1, f32[32,2048]{1,0:T(8,128)} %bitcast.5, f32[32,1024]{1,0:T(8,128)} %bitcast.6), custom_call_target="tpu_custom_call" | custom-call | tf_op jit(solution)/shard_map/sinkhorn/pallas_call | solution.py:303
  57.7 1.3 %outputs.1 = (f32[32,2048]{1,0:T(8,128)}, f32[32,1024]{1,0:T(8,128)}, f32[1,32]{1,0:T(1,128)}) custom-call(f32[32,2048]{1,0:T(8,128)S(1)} %get-tuple-element.9.refs_0_, f32[32,1024]{1,0:T(8,128)S(1)} %get-tuple-element.10.refs_1_, f32[8,1,128]{2,1,0:T(1,128)S(1)} %get-tuple-element.11.refs_2_), custom_call_target="tpu_custom_call" | custom-call | tf_op jit(solution)/shard_map/outputs/pallas_call | solution.py:330

commit v17 on v16

--- a/solution.py
+++ b/solution.py
@@ -7,7 +7,7 @@
 
 SWEEPS = 6
 AHEAD = (8, 7)
-WAIT_NS = ((0, 350), (650, 600))
+WAIT_NS = ((0, 700), (650, 600))
 F32 = jnp.float32
 BF16 = jnp.bfloat16
 MESH = pl.DeviceIdType.MESH

time: 59.1 us -> 59.8 us (1.012)
  Pallas kernels: 58.4 us -> 59.1 us
    pallas_call x1, Pallas kernels: 57.1 us -> 57.8 us  [local_fn(): pl.pallas_call(lambda *refs: sinkhorn_kernel(n_chunk, *refs), out_shape=(...]
where the time goes in v17:
time: 59.8 us; the launch traced here: 59.7 us
  Pallas kernels  59.1 us (99%)
  between operations  0.64 us (1%)
    pallas_call x1, Pallas kernels, local_fn(): pl.pallas_call(lambda *refs: sinkhorn_kernel(n_chunk, *refs), out_shape=(...  57.8 us
    pallas_call x1, Pallas kernels, local_fn(): pl.pallas_call(lambda *refs: output_kernel(norm, *refs), out_shape=(jax.S...  1.27 us

profile of v17, /device:TPU:0, one launch (start us, length us, event | category | flops | bytes accessed | tf_op | source)
XLA Modules:
  0.0 59.7 jit_solution(10292796018350874385)
XLA Ops:
  0.6 57.8 %sinkhorn.1 = (f32[32,2048]{1,0:T(8,128)S(1)}, f32[32,1024]{1,0:T(8,128)S(1)}, f32[8,1,128]{2,1,0:T(1,128)S(1)}) custom-call(bf16[2048,1024]{1,0:T(8,128)(2,1)} %refs_0_.1, bf16[2048,1024]{1,0:T(8,128)(2,1)} %refs_1_.1, f32[32,2048]{1,0:T(8,128)} %bitcast.5, f32[32,1024]{1,0:T(8,128)} %bitcast.6), custom_call_target="tpu_custom_call" | custom-call | tf_op jit(solution)/shard_map/sinkhorn/pallas_call | solution.py:303
  58.4 1.3 %outputs.1 = (f32[32,2048]{1,0:T(8,128)}, f32[32,1024]{1,0:T(8,128)}, f32[1,32]{1,0:T(1,128)}) custom-call(f32[32,2048]{1,0:T(8,128)S(1)} %get-tuple-element.9.refs_0_, f32[32,1024]{1,0:T(8,128)S(1)} %get-tuple-element.10.refs_1_, f32[8,1,128]{2,1,0:T(1,128)S(1)} %get-tuple-element.11.refs_2_), custom_call_target="tpu_custom_call" | custom-call | tf_op jit(solution)/shard_map/outputs/pallas_call | solution.py:330

commit v18 on v17

--- a/solution.py
+++ b/solution.py
@@ -7,7 +7,7 @@
 
 SWEEPS = 6
 AHEAD = (8, 7)
-WAIT_NS = ((0, 700), (650, 600))
+WAIT_NS = ((0, 350), (550, 400))
 F32 = jnp.float32
 BF16 = jnp.bfloat16
 MESH = pl.DeviceIdType.MESH

time: 59.8 us -> 60.4 us (1.010)
  no operation moved by 1% of the time
where the time goes in v18:
time: 60.4 us; the launch traced here: 60.3 us
  Pallas kernels  59.7 us (99%)
  between operations  0.64 us (1%)
    pallas_call x1, Pallas kernels, local_fn(): pl.pallas_call(lambda *refs: sinkhorn_kernel(n_chunk, *refs), out_shape=(...  58.4 us
    pallas_call x1, Pallas kernels, local_fn(): pl.pallas_call(lambda *refs: output_kernel(norm, *refs), out_shape=(jax.S...  1.27 us

profile of v18, /device:TPU:0, one launch (start us, length us, event | category | flops | bytes accessed | tf_op | source)
XLA Modules:
  0.0 60.3 jit_solution(17030657937091594579)
XLA Ops:
  0.6 58.4 %sinkhorn.1 = (f32[32,2048]{1,0:T(8,128)S(1)}, f32[32,1024]{1,0:T(8,128)S(1)}, f32[8,1,128]{2,1,0:T(1,128)S(1)}) custom-call(bf16[2048,1024]{1,0:T(8,128)(2,1)} %refs_0_.1, bf16[2048,1024]{1,0:T(8,128)(2,1)} %refs_1_.1, f32[32,2048]{1,0:T(8,128)} %bitcast.5, f32[32,1024]{1,0:T(8,128)} %bitcast.6), custom_call_target="tpu_custom_call" | custom-call | tf_op jit(solution)/shard_map/sinkhorn/pallas_call | solution.py:303
  59.0 1.3 %outputs.1 = (f32[32,2048]{1,0:T(8,128)}, f32[32,1024]{1,0:T(8,128)}, f32[1,32]{1,0:T(1,128)}) custom-call(f32[32,2048]{1,0:T(8,128)S(1)} %get-tuple-element.9.refs_0_, f32[32,1024]{1,0:T(8,128)S(1)} %get-tuple-element.10.refs_1_, f32[8,1,128]{2,1,0:T(1,128)S(1)} %get-tuple-element.11.refs_2_), custom_call_target="tpu_custom_call" | custom-call | tf_op jit(solution)/shard_map/outputs/pallas_call | solution.py:330

commit v19 on v18

--- a/solution.py
+++ b/solution.py
@@ -7,7 +7,7 @@
 
 SWEEPS = 6
 AHEAD = (8, 7)
-WAIT_NS = ((0, 350), (550, 400))
+WAIT_NS = ((0, 0), (300, 250))
 F32 = jnp.float32
 BF16 = jnp.bfloat16
 MESH = pl.DeviceIdType.MESH
@@ -155,7 +155,7 @@
     for i in range(n_chunk):
         all_here(k_buf.at[1 - core, krows(i)], kp_recv.at[i])
         transpose_rows(1 - core, i)
-        if i == 0:
+        if i == 1:
             for n in range(per_half):
                 t0_send(1, n)
 

time: 60.4 us -> 58.8 us (0.974)
  Pallas kernels: 59.7 us -> 58.1 us
    pallas_call x1, Pallas kernels: 58.4 us -> 56.8 us  [local_fn(): pl.pallas_call(lambda *refs: sinkhorn_kernel(n_chunk, *refs), out_shape=(...]
where the time goes in v19:
time: 58.8 us; the launch traced here: 58.7 us
  Pallas kernels  58.1 us (99%)
  between operations  0.64 us (1%)
    pallas_call x1, Pallas kernels, local_fn(): pl.pallas_call(lambda *refs: sinkhorn_kernel(n_chunk, *refs), out_shape=(...  56.8 us
    pallas_call x1, Pallas kernels, local_fn(): pl.pallas_call(lambda *refs: output_kernel(norm, *refs), out_shape=(jax.S...  1.27 us

profile of v19, /device:TPU:0, one launch (start us, length us, event | category | flops | bytes accessed | tf_op | source)
XLA Modules:
  0.0 58.7 jit_solution(11168708067395043180)
XLA Ops:
  0.6 56.8 %sinkhorn.1 = (f32[32,2048]{1,0:T(8,128)S(1)}, f32[32,1024]{1,0:T(8,128)S(1)}, f32[8,1,128]{2,1,0:T(1,128)S(1)}) custom-call(bf16[2048,1024]{1,0:T(8,128)(2,1)} %refs_0_.1, bf16[2048,1024]{1,0:T(8,128)(2,1)} %refs_1_.1, f32[32,2048]{1,0:T(8,128)} %bitcast.5, f32[32,1024]{1,0:T(8,128)} %bitcast.6), custom_call_target="tpu_custom_call" | custom-call | tf_op jit(solution)/shard_map/sinkhorn/pallas_call | solution.py:303
  57.5 1.3 %outputs.1 = (f32[32,2048]{1,0:T(8,128)}, f32[32,1024]{1,0:T(8,128)}, f32[1,32]{1,0:T(1,128)}) custom-call(f32[32,2048]{1,0:T(8,128)S(1)} %get-tuple-element.9.refs_0_, f32[32,1024]{1,0:T(8,128)S(1)} %get-tuple-element.10.refs_1_, f32[8,1,128]{2,1,0:T(1,128)S(1)} %get-tuple-element.11.refs_2_), custom_call_target="tpu_custom_call" | custom-call | tf_op jit(solution)/shard_map/outputs/pallas_call | solution.py:330

commit v20 on v19

--- a/solution.py
+++ b/solution.py
@@ -6,8 +6,8 @@
 from jax.sharding import PartitionSpec as P
 
 SWEEPS = 6
-AHEAD = (8, 7)
-WAIT_NS = ((0, 0), (300, 250))
+AHEAD = (8, 6)
+WAIT_NS = ((0, 0), (200, 200))
 F32 = jnp.float32
 BF16 = jnp.bfloat16
 MESH = pl.DeviceIdType.MESH

time: 58.8 us -> 62.1 us (1.056)
  Pallas kernels: 58.1 us -> 61.4 us
    pallas_call x1, Pallas kernels: 56.8 us -> 60.1 us  [local_fn(): pl.pallas_call(lambda *refs: sinkhorn_kernel(n_chunk, *refs), out_shape=(...]
where the time goes in v20:
time: 62.1 us; the launch traced here: 62 us
  Pallas kernels  61.4 us (99%)
  between operations  0.64 us (1%)
    pallas_call x1, Pallas kernels, local_fn(): pl.pallas_call(lambda *refs: sinkhorn_kernel(n_chunk, *refs), out_shape=(...  60.1 us
    pallas_call x1, Pallas kernels, local_fn(): pl.pallas_call(lambda *refs: output_kernel(norm, *refs), out_shape=(jax.S...  1.27 us

profile of v20, /device:TPU:0, one launch (start us, length us, event | category | flops | bytes accessed | tf_op | source)
XLA Modules:
  0.0 62.0 jit_solution(1911740003620439198)
XLA Ops:
  0.6 60.1 %sinkhorn.1 = (f32[32,2048]{1,0:T(8,128)S(1)}, f32[32,1024]{1,0:T(8,128)S(1)}, f32[8,1,128]{2,1,0:T(1,128)S(1)}) custom-call(bf16[2048,1024]{1,0:T(8,128)(2,1)} %refs_0_.1, bf16[2048,1024]{1,0:T(8,128)(2,1)} %refs_1_.1, f32[32,2048]{1,0:T(8,128)} %bitcast.5, f32[32,1024]{1,0:T(8,128)} %bitcast.6), custom_call_target="tpu_custom_call" | custom-call | tf_op jit(solution)/shard_map/sinkhorn/pallas_call | solution.py:303
  60.7 1.3 %outputs.1 = (f32[32,2048]{1,0:T(8,128)}, f32[32,1024]{1,0:T(8,128)}, f32[1,32]{1,0:T(1,128)}) custom-call(f32[32,2048]{1,0:T(8,128)S(1)} %get-tuple-element.9.refs_0_, f32[32,1024]{1,0:T(8,128)S(1)} %get-tuple-element.10.refs_1_, f32[8,1,128]{2,1,0:T(1,128)S(1)} %get-tuple-element.11.refs_2_), custom_call_target="tpu_custom_call" | custom-call | tf_op jit(solution)/shard_map/outputs/pallas_call | solution.py:330

commit v21 on v19

--- a/solution.py
+++ b/solution.py
@@ -7,7 +7,7 @@
 
 SWEEPS = 6
 AHEAD = (8, 7)
-WAIT_NS = ((0, 0), (300, 250))
+WAIT_NS = ((0, 0), (450, 400))
 F32 = jnp.float32
 BF16 = jnp.bfloat16
 MESH = pl.DeviceIdType.MESH

time: 58.8 us -> 58.9 us (level)
  no operation moved by 1% of the time
where the time goes in v21:
time: 58.9 us; the launch traced here: 58.8 us
  Pallas kernels  58.2 us (99%)
  between operations  0.64 us (1%)
    pallas_call x1, Pallas kernels, local_fn(): pl.pallas_call(lambda *refs: sinkhorn_kernel(n_chunk, *refs), out_shape=(...  56.9 us
    pallas_call x1, Pallas kernels, local_fn(): pl.pallas_call(lambda *refs: output_kernel(norm, *refs), out_shape=(jax.S...  1.27 us

profile of v21, /device:TPU:0, one launch (start us, length us, event | category | flops | bytes accessed | tf_op | source)
XLA Modules:
  0.0 58.8 jit_solution(74282172975319351)
XLA Ops:
  0.6 56.9 %sinkhorn.1 = (f32[32,2048]{1,0:T(8,128)S(1)}, f32[32,1024]{1,0:T(8,128)S(1)}, f32[8,1,128]{2,1,0:T(1,128)S(1)}) custom-call(bf16[2048,1024]{1,0:T(8,128)(2,1)} %refs_0_.1, bf16[2048,1024]{1,0:T(8,128)(2,1)} %refs_1_.1, f32[32,2048]{1,0:T(8,128)} %bitcast.5, f32[32,1024]{1,0:T(8,128)} %bitcast.6), custom_call_target="tpu_custom_call" | custom-call | tf_op jit(solution)/shard_map/sinkhorn/pallas_call | solution.py:303
  57.6 1.3 %outputs.1 = (f32[32,2048]{1,0:T(8,128)}, f32[32,1024]{1,0:T(8,128)}, f32[1,32]{1,0:T(1,128)}) custom-call(f32[32,2048]{1,0:T(8,128)S(1)} %get-tuple-element.9.refs_0_, f32[32,1024]{1,0:T(8,128)S(1)} %get-tuple-element.10.refs_1_, f32[8,1,128]{2,1,0:T(1,128)S(1)} %get-tuple-element.11.refs_2_), custom_call_target="tpu_custom_call" | custom-call | tf_op jit(solution)/shard_map/outputs/pallas_call | solution.py:330

commit v22 on v21

--- a/solution.py
+++ b/solution.py
@@ -7,7 +7,7 @@
 
 SWEEPS = 6
 AHEAD = (8, 7)
-WAIT_NS = ((0, 0), (450, 400))
+WAIT_NS = ((0, 0), (450, 250))
 F32 = jnp.float32
 BF16 = jnp.bfloat16
 MESH = pl.DeviceIdType.MESH

time: 58.9 us -> 58.7 us (level)
  no operation moved by 1% of the time
where the time goes in v22:
time: 58.7 us; the launch traced here: 58.6 us
  Pallas kernels  58 us (99%)
  between operations  0.64 us (1%)
    pallas_call x1, Pallas kernels, local_fn(): pl.pallas_call(lambda *refs: sinkhorn_kernel(n_chunk, *refs), out_shape=(...  56.7 us
    pallas_call x1, Pallas kernels, local_fn(): pl.pallas_call(lambda *refs: output_kernel(norm, *refs), out_shape=(jax.S...  1.27 us

profile of v22, /device:TPU:0, one launch (start us, length us, event | category | flops | bytes accessed | tf_op | source)
XLA Modules:
  0.0 58.6 jit_solution(10240997597067905606)
XLA Ops:
  0.6 56.7 %sinkhorn.1 = (f32[32,2048]{1,0:T(8,128)S(1)}, f32[32,1024]{1,0:T(8,128)S(1)}, f32[8,1,128]{2,1,0:T(1,128)S(1)}) custom-call(bf16[2048,1024]{1,0:T(8,128)(2,1)} %refs_0_.1, bf16[2048,1024]{1,0:T(8,128)(2,1)} %refs_1_.1, f32[32,2048]{1,0:T(8,128)} %bitcast.5, f32[32,1024]{1,0:T(8,128)} %bitcast.6), custom_call_target="tpu_custom_call" | custom-call | tf_op jit(solution)/shard_map/sinkhorn/pallas_call | solution.py:303
  57.3 1.3 %outputs.1 = (f32[32,2048]{1,0:T(8,128)}, f32[32,1024]{1,0:T(8,128)}, f32[1,32]{1,0:T(1,128)}) custom-call(f32[32,2048]{1,0:T(8,128)S(1)} %get-tuple-element.9.refs_0_, f32[32,1024]{1,0:T(8,128)S(1)} %get-tuple-element.10.refs_1_, f32[8,1,128]{2,1,0:T(1,128)S(1)} %get-tuple-element.11.refs_2_), custom_call_target="tpu_custom_call" | custom-call | tf_op jit(solution)/shard_map/outputs/pallas_call | solution.py:330

commit v23 on v22

--- a/solution.py
+++ b/solution.py
@@ -7,7 +7,7 @@
 
 SWEEPS = 6
 AHEAD = (8, 7)
-WAIT_NS = ((0, 0), (450, 250))
+WAIT_NS = ((0, 0), (600, 250))
 F32 = jnp.float32
 BF16 = jnp.bfloat16
 MESH = pl.DeviceIdType.MESH

time: 58.7 us -> 58.7 us (level)
  no operation moved by 1% of the time
where the time goes in v23:
time: 58.7 us; the launch traced here: 58.6 us
  Pallas kernels  58 us (99%)
  between operations  0.64 us (1%)
    pallas_call x1, Pallas kernels, local_fn(): pl.pallas_call(lambda *refs: sinkhorn_kernel(n_chunk, *refs), out_shape=(...  56.7 us
    pallas_call x1, Pallas kernels, local_fn(): pl.pallas_call(lambda *refs: output_kernel(norm, *refs), out_shape=(jax.S...  1.27 us

profile of v23, /device:TPU:0, one launch (start us, length us, event | category | flops | bytes accessed | tf_op | source)
XLA Modules:
  0.0 58.6 jit_solution(13304893623094008515)
XLA Ops:
  0.6 56.7 %sinkhorn.1 = (f32[32,2048]{1,0:T(8,128)S(1)}, f32[32,1024]{1,0:T(8,128)S(1)}, f32[8,1,128]{2,1,0:T(1,128)S(1)}) custom-call(bf16[2048,1024]{1,0:T(8,128)(2,1)} %refs_0_.1, bf16[2048,1024]{1,0:T(8,128)(2,1)} %refs_1_.1, f32[32,2048]{1,0:T(8,128)} %bitcast.5, f32[32,1024]{1,0:T(8,128)} %bitcast.6), custom_call_target="tpu_custom_call" | custom-call | tf_op jit(solution)/shard_map/sinkhorn/pallas_call | solution.py:303
  57.3 1.3 %outputs.1 = (f32[32,2048]{1,0:T(8,128)}, f32[32,1024]{1,0:T(8,128)}, f32[1,32]{1,0:T(1,128)}) custom-call(f32[32,2048]{1,0:T(8,128)S(1)} %get-tuple-element.9.refs_0_, f32[32,1024]{1,0:T(8,128)S(1)} %get-tuple-element.10.refs_1_, f32[8,1,128]{2,1,0:T(1,128)S(1)} %get-tuple-element.11.refs_2_), custom_call_target="tpu_custom_call" | custom-call | tf_op jit(solution)/shard_map/outputs/pallas_call | solution.py:330

commit v24 on v23

--- a/solution.py
+++ b/solution.py
@@ -7,7 +7,7 @@
 
 SWEEPS = 6
 AHEAD = (8, 7)
-WAIT_NS = ((0, 0), (600, 250))
+WAIT_NS = ((0, 150), (450, 250))
 F32 = jnp.float32
 BF16 = jnp.bfloat16
 MESH = pl.DeviceIdType.MESH

time: 58.7 us -> 59 us (level)
  no operation moved by 1% of the time
where the time goes in v24:
time: 59 us; the launch traced here: 58.9 us
  Pallas kernels  58.3 us (99%)
  between operations  0.64 us (1%)
    pallas_call x1, Pallas kernels, local_fn(): pl.pallas_call(lambda *refs: sinkhorn_kernel(n_chunk, *refs), out_shape=(...  57 us
    pallas_call x1, Pallas kernels, local_fn(): pl.pallas_call(lambda *refs: output_kernel(norm, *refs), out_shape=(jax.S...  1.27 us

profile of v24, /device:TPU:0, one launch (start us, length us, event | category | flops | bytes accessed | tf_op | source)
XLA Modules:
  0.0 58.9 jit_solution(137910082875176033)
XLA Ops:
  0.6 57.0 %sinkhorn.1 = (f32[32,2048]{1,0:T(8,128)S(1)}, f32[32,1024]{1,0:T(8,128)S(1)}, f32[8,1,128]{2,1,0:T(1,128)S(1)}) custom-call(bf16[2048,1024]{1,0:T(8,128)(2,1)} %refs_0_.1, bf16[2048,1024]{1,0:T(8,128)(2,1)} %refs_1_.1, f32[32,2048]{1,0:T(8,128)} %bitcast.5, f32[32,1024]{1,0:T(8,128)} %bitcast.6), custom_call_target="tpu_custom_call" | custom-call | tf_op jit(solution)/shard_map/sinkhorn/pallas_call | solution.py:303
  57.6 1.3 %outputs.1 = (f32[32,2048]{1,0:T(8,128)}, f32[32,1024]{1,0:T(8,128)}, f32[1,32]{1,0:T(1,128)}) custom-call(f32[32,2048]{1,0:T(8,128)S(1)} %get-tuple-element.9.refs_0_, f32[32,1024]{1,0:T(8,128)S(1)} %get-tuple-element.10.refs_1_, f32[8,1,128]{2,1,0:T(1,128)S(1)} %get-tuple-element.11.refs_2_), custom_call_target="tpu_custom_call" | custom-call | tf_op jit(solution)/shard_map/outputs/pallas_call | solution.py:330

commit v25 on v24

--- a/solution.py
+++ b/solution.py
@@ -7,7 +7,7 @@
 
 SWEEPS = 6
 AHEAD = (8, 7)
-WAIT_NS = ((0, 150), (450, 250))
+WAIT_NS = ((0, 0), (500, 180))
 F32 = jnp.float32
 BF16 = jnp.bfloat16
 MESH = pl.DeviceIdType.MESH

time: 59 us -> 59 us (level)
  no operation moved by 1% of the time
where the time goes in v25:
time: 59 us; the launch traced here: 58.9 us
  Pallas kernels  58.3 us (99%)
  between operations  0.64 us (1%)
    pallas_call x1, Pallas kernels, local_fn(): pl.pallas_call(lambda *refs: sinkhorn_kernel(n_chunk, *refs), out_shape=(...  57 us
    pallas_call x1, Pallas kernels, local_fn(): pl.pallas_call(lambda *refs: output_kernel(norm, *refs), out_shape=(jax.S...  1.27 us

profile of v25, /device:TPU:0, one launch (start us, length us, event | category | flops | bytes accessed | tf_op | source)
XLA Modules:
  0.0 58.9 jit_solution(288816365418215465)
XLA Ops:
  0.6 57.0 %sinkhorn.1 = (f32[32,2048]{1,0:T(8,128)S(1)}, f32[32,1024]{1,0:T(8,128)S(1)}, f32[8,1,128]{2,1,0:T(1,128)S(1)}) custom-call(bf16[2048,1024]{1,0:T(8,128)(2,1)} %refs_0_.1, bf16[2048,1024]{1,0:T(8,128)(2,1)} %refs_1_.1, f32[32,2048]{1,0:T(8,128)} %bitcast.5, f32[32,1024]{1,0:T(8,128)} %bitcast.6), custom_call_target="tpu_custom_call" | custom-call | tf_op jit(solution)/shard_map/sinkhorn/pallas_call | solution.py:303
  57.7 1.3 %outputs.1 = (f32[32,2048]{1,0:T(8,128)}, f32[32,1024]{1,0:T(8,128)}, f32[1,32]{1,0:T(1,128)}) custom-call(f32[32,2048]{1,0:T(8,128)S(1)} %get-tuple-element.9.refs_0_, f32[32,1024]{1,0:T(8,128)S(1)} %get-tuple-element.10.refs_1_, f32[8,1,128]{2,1,0:T(1,128)S(1)} %get-tuple-element.11.refs_2_), custom_call_target="tpu_custom_call" | custom-call | tf_op jit(solution)/shard_map/outputs/pallas_call | solution.py:330

commit v26 on v15

--- a/solution.py
+++ b/solution.py
@@ -165,7 +165,7 @@
 
     @pl.when(grp == 1)
     def _():
-        pl.delay(WAIT_NS)
+        pl.delay(WAIT_NS + (1 - core) * 100)
 
     all_here(t0_buf.at[0], one_recv.at[2])
     order = list(range(per_half, n_chunk)) + list(range(per_half))

time: 58.6 us -> 58.5 us (level)
  no operation moved by 1% of the time
where the time goes in v26:
time: 58.5 us; the launch traced here: 58.4 us
  Pallas kernels  57.8 us (99%)
  between operations  0.64 us (1%)
    pallas_call x1, Pallas kernels, local_fn(): pl.pallas_call(lambda *refs: sinkhorn_kernel(n_chunk, *refs), out_shape=(...  56.5 us
    pallas_call x1, Pallas kernels, local_fn(): pl.pallas_call(lambda *refs: output_kernel(norm, *refs), out_shape=(jax.S...  1.27 us

profile of v26, /device:TPU:0, one launch (start us, length us, event | category | flops | bytes accessed | tf_op | source)
XLA Modules:
  0.0 58.4 jit_solution(13122900484569106966)
XLA Ops:
  0.6 56.5 %sinkhorn.1 = (f32[32,2048]{1,0:T(8,128)S(1)}, f32[32,1024]{1,0:T(8,128)S(1)}, f32[8,1,128]{2,1,0:T(1,128)S(1)}) custom-call(bf16[2048,1024]{1,0:T(8,128)(2,1)} %refs_0_.1, bf16[2048,1024]{1,0:T(8,128)(2,1)} %refs_1_.1, f32[32,2048]{1,0:T(8,128)} %bitcast.5, f32[32,1024]{1,0:T(8,128)} %bitcast.6), custom_call_target="tpu_custom_call" | custom-call | tf_op jit(solution)/shard_map/sinkhorn/pallas_call | solution.py:300
  57.2 1.3 %outputs.1 = (f32[32,2048]{1,0:T(8,128)}, f32[32,1024]{1,0:T(8,128)}, f32[1,32]{1,0:T(1,128)}) custom-call(f32[32,2048]{1,0:T(8,128)S(1)} %get-tuple-element.9.refs_0_, f32[32,1024]{1,0:T(8,128)S(1)} %get-tuple-element.10.refs_1_, f32[8,1,128]{2,1,0:T(1,128)S(1)} %get-tuple-element.11.refs_2_), custom_call_target="tpu_custom_call" | custom-call | tf_op jit(solution)/shard_map/outputs/pallas_call | solution.py:327
